TPU v7x, 32 devices: a whole 2x2x4 slice. The times are simulated.
32 devices in a mesh: dp: 4 (over y, x), tensor: 8 (over z, core).
Axes of the slice: x: 2, y: 2, z: 4, core: 2. Of those that a mesh axis runs over, the one named last changes fastest.
Arguments:
- logits: bfloat16 [1024, 152064], P('dp', 'tensor'), may hold values from -120 to 256
- child_ids: int32 [1024, 64], P('dp'), may hold values from 0 to 152063
- leaf_counts: int32 [1024, 64], P('dp'), may hold values from 1 to 1024
- leaf_valid: int32 [1024], P('dp'), may hold values from 1 to 64
- leaf_temp: float32 [1024], P('dp'), may hold values from 0.5 to 2
- leaf_owner: int32 [1024], P('dp'), may hold values from 0 to 1023, as said below
Outputs:
- gradient: bfloat16 [1024, 152064], P('dp', 'tensor')
- row_loss: float32 [1024], P('dp')
- mean_loss: float32 [], replicated
Inputs may be any that keep to these rules, and one draw needn't show every extreme that they name: `leaf_owner`: every position is named by exactly one leaf row. Of the leaf rows of one dp index, exactly 64 name positions of each owner index.
All inputs are finite; a program needn't handle non-finite values.
Results may differ from a plain program's by a relative error of at most 0.001.
Values may be sent and summed in bfloat16 or wider, within the bound.
No kernel may reach another device: no remote copies, remote signals or barrier semaphores. Data moves between devices by JAX's collectives and lax.ppermute only.
A program may use at most 64 MiB of HBM per device.

v0:
```python
import jax
import jax.numpy as jnp
from jax import lax
from jax.sharding import PartitionSpec as P


def select_rows(matcher, values):
    return jnp.dot(
        matcher, values, preferred_element_type=jnp.float32, precision=lax.Precision.HIGHEST
    )


def body(logits, child_ids, leaf_counts, leaf_valid, leaf_temp, leaf_owner):
    pos_dev = logits.shape[0]
    columns_dev = logits.shape[1]
    children = leaf_counts.shape[1]
    groups = lax.axis_size("dp")
    slot_index = jnp.arange(children, dtype=jnp.int32)
    in_use = slot_index[None, :] < leaf_valid[:, None]
    powered = jnp.exp(jnp.log(leaf_counts.astype(jnp.float32)) * leaf_temp[:, None])
    weights = jnp.where(in_use, powered, jnp.float32(0.0))
    owner_dev = leaf_owner // pos_dev
    local_slot = leaf_owner % pos_dev
    onehot = (owner_dev[:, None] == jnp.arange(groups, dtype=jnp.int32)[None, :]).astype(jnp.int32)
    slot_rank = jnp.sum((jnp.cumsum(onehot, axis=0) - onehot) * onehot, axis=1)
    capacity = pos_dev // groups
    destination = owner_dev * capacity + slot_rank
    send_index = jnp.arange(groups * capacity, dtype=jnp.int32)
    sender = send_index[:, None] == destination[None, :]
    outgoing = select_rows(sender.astype(jnp.float32), weights).reshape(groups, capacity, children)
    labels = jnp.sum(jnp.where(sender, local_slot[None, :], 0), axis=1).reshape(groups, capacity)
    incoming, incoming_labels = (
        lax.all_to_all(outgoing, "dp", split_axis=0, concat_axis=0, tiled=True),
        lax.all_to_all(labels, "dp", split_axis=0, concat_axis=0, tiled=True),
    )
    receive_slot = incoming_labels.reshape(-1)
    receiver = (jnp.arange(pos_dev, dtype=jnp.int32)[:, None] == receive_slot[None, :]).astype(
        jnp.float32
    )
    placed = select_rows(receiver, incoming.reshape(-1, children))
    targets = placed / jnp.sum(placed, axis=1)[:, None]
    column_start = lax.axis_index("tensor") * columns_dev
    local_ids = child_ids - column_start
    column_index = jnp.arange(columns_dev, dtype=jnp.int32)
    matches = local_ids[:, None, :] == column_index[None, :, None]
    target_dense = jnp.sum(jnp.where(matches, targets[:, None, :], jnp.float32(0.0)), axis=2)
    values = logits.astype(jnp.float32)
    picked_part = jnp.sum(target_dense * values, axis=1)
    own_top_narrow = jnp.max(logits, axis=1)
    row_top = lax.pmax(own_top_narrow, "tensor").astype(jnp.float32)
    own_sum = jnp.sum(jnp.exp(values - row_top[:, None]), axis=1)
    sumexp, picked = lax.psum((own_sum, picked_part), "tensor")
    row_loss = row_top + jnp.log(sumexp) - picked
    scale = 1.0 / sumexp
    gradient = (jnp.exp(values - row_top[:, None]) * scale[:, None] - target_dense).astype(
        jnp.bfloat16
    )
    loss_sum = lax.psum(jnp.sum(row_loss), "dp")
    mean_loss = loss_sum / (groups * pos_dev)
    return (gradient, row_loss, mean_loss)


def solution(mesh):
    return jax.shard_map(
        body,
        mesh=mesh,
        in_specs=(P("dp", "tensor"), P("dp", None), P("dp", None), P("dp"), P("dp"), P("dp")),
        out_specs=(P("dp", "tensor"), P("dp"), P()),
        check_vma=False,
    )
```

profile of v0, /device:TPU:0, one launch (start us, length us, event | category | flops | bytes accessed | tf_op | source)
XLA Modules:
  0.0 426.2 jit_solution(4573471683408045461)
XLA Ops:
  0.6 0.7 and_select_fusion
  1.3 1.2 reduce-window.6
  2.6 0.1 slice.8
  2.6 0.1 copy.24
  2.8 0.1 copy.25
  2.9 0.1 add_bitcast_fusion
  3.0 0.1 select_reduce_fusion.1
  3.1 0.7 all_to_all.9
  3.8 5.2 %all-to-all-start = ((s32[4,1,64]{2,1,0:T(1,128)}), s32[4,1,64]{2,1,0:T(1,128)S(1)}, u32[]{:S(2)}, u32[]{:S(2)}) async-start(s32[4,1,64]{2,1,0:T(1,128)} %all_to_all.9), calls=%async_computation | async-start | bytes 4096 | tf_op jit(solution)/shard_map/all_to_all | solution.py:34
  9.0 1.1 fusion.6
  10.1 0.1 reshape.44
  10.2 0.8 reshape.55
  11.0 2.5 all-to-all-done
  13.5 3.3 all-to-all-start.1
  16.8 0.8 broadcast_subtract_fusion
  17.6 6.2 %reduce_max.9 = bf16[256]{0:T(256)(128)(2,1)S(1)} reduce(bf16[256,19008]{0,1:T(8,128)(2,1)} %param.6, bf16[]{:T(256)} %constant.37.clone.1), dimensions={1}, to_apply=%region_0.1 | reduce | flops 4865792 | bytes 9732610 | tf_op jit(solution)/shard_map/reduce_max | solution.py:49
  23.9 15.4 %pmax.7 = bf16[256]{0:T(256)(128)(2,1)S(1)} all-reduce(bf16[256]{0:T(256)(128)(2,1)S(1)} %reduce_max.9), channel_id=1, replica_groups=mesh['dp'=4,'tensor'=8] {'tensor'}, use_global_device_ids=true, to_apply=%region_1.2 | all-reduce | flops 256 | bytes 1024 | tf_op jit(solution)/shard_map/pmax | solution.py:50
  39.2 0.5 broadcast.64
  39.8 0.7 reduce.3
  40.4 0.1 eq.80
  40.5 0.5 broadcast.65
  41.0 0.8 reduce.4
  41.8 0.1 reshape.56
  42.0 0.1 copy.27
  42.1 0.1 reshape.45
  42.2 0.3 fusion.23
  42.5 330.2 %select_reduce_fusion = f32[256,19008]{0,1:T(8,128)} fusion(f32[256,64]{0,1:T(8,128)S(1)} %broadcast_divide_fusion, s32[256,64]{0,1:T(8,128)S(1)} %broadcast_subtract_fusion), kind=kLoop, calls=%fused_computation | loop fusion | flops 929415168 | bytes 19595264 | tf_op jit(solution)/shard_map/reduce_sum | solution.py:46
  372.7 11.3 %fusion.5 = (f32[256]{0:T(256)S(1)}, f32[256]{0:T(256)S(1)}) fusion(f32[256,19008]{0,1:T(8,128)} %select_reduce_fusion, bf16[256,19008]{0,1:T(8,128)(2,1)} %param.6, f32[256]{0:T(256)S(1)} %convert_element_type.22), kind=kLoop, calls=%fused_computation.9 | loop fusion | flops 24329728 | bytes 29199360 | tf_op jit(solution)/shard_map/reduce_sum | solution.py:48
  384.0 13.6 %all-reduce = (f32[256]{0:T(256)S(1)}, f32[256]{0:T(256)S(1)}) all-reduce(f32[256]{0:T(256)S(1)} %get-tuple-element.4, f32[256]{0:T(256)S(1)} %get-tuple-element.3), channel_id=1, replica_groups=mesh['dp'=4,'tensor'=8] {'tensor'}, use_global_device_ids=true, to_apply=%region_3.4 | all-reduce | flops 512 | bytes 4096 | tf_op jit(solution)/shard_map/psum | solution.py:52
  397.6 1.2 fusion.22
  398.8 10.7 %psum.23 = f32[]{:T(128)} all-reduce(f32[]{:T(128)} %get-tuple-element.7), channel_id=1, replica_groups=mesh['dp'=4,'tensor'=8] {'dp'}, use_global_device_ids=true, to_apply=%region_13.14 | all-reduce | flops 1 | bytes 8 | tf_op jit(solution)/shard_map/psum | solution.py:58
  409.5 15.0 %fusion.4 = bf16[256,19008]{0,1:T(8,128)(2,1)} fusion(f32[256,19008]{0,1:T(8,128)} %select_reduce_fusion, bf16[256,19008]{0,1:T(8,128)(2,1)} %param.6, f32[256]{0:T(256)S(1)} %get-tuple-element.9, f32[256]{0:T(256)S(1)} %convert_element_type.22), kind=kLoop, calls=%fused_computation.8 | loop fusion | flops 24330240 | bytes 38930432 | tf_op jit(solution)/shard_map/convert_element_type | solution.py:55
  (9 shorter events, 0.1 us)
Async XLA Ops:
  3.8 9.7 %all-to-all-start = ((s32[4,1,64]{2,1,0:T(1,128)}), s32[4,1,64]{2,1,0:T(1,128)S(1)}, u32[]{:S(2)}, u32[]{:S(2)}) async-start(s32[4,1,64]{2,1,0:T(1,128)} %all_to_all.9), calls=%async_computation | async-start | bytes 4096 | tf_op jit(solution)/shard_map/all_to_all | solution.py:34
  13.5 27.0 %all-to-all-start.1 = ((f32[4,1,4096]{2,1,0:T(1,128)}), f32[4,1,4096]{2,1,0:T(1,128)S(1)}, u32[]{:S(2)}, u32[]{:S(2)}) async-start(f32[4,1,4096]{2,1,0:T(1,128)} %reshape.55), calls=%async_computation.1 | async-start | bytes 131072 | tf_op jit(solution)/shard_map/all_to_all | solution.py:33
where the time goes:
time: 427 us; the launch traced here: 426 us
  other arithmetic  368 us (86%)
  blocking collectives  39.6 us (9%)
  starting transfers between devices  8.48 us (2%)
    reduce_sum x1, other arithmetic, body(): jnp.sum(jnp.where(matches, targets[:, None, :], jnp.float32(0.0)), axis=2)  330 us
    pmax x1, blocking collectives, body(): row_top = lax.pmax(own_top_narrow, 'tensor').astype(jnp.float32)  15.4 us
    convert_element_type x1, other arithmetic, body(): (jnp.exp(values - row_top[:, None]) * scale[:, None] - target_dense).asty...  15 us
    psum x1, blocking collectives, body(): sumexp, picked = lax.psum((own_sum, picked_part), 'tensor')  13.6 us
    reduce_sum x1, other arithmetic, body(): picked_part = jnp.sum(target_dense * values, axis=1)  11.3 us
    psum x1, blocking collectives, body(): loss_sum = lax.psum(jnp.sum(row_loss), 'dp')  10.7 us
  transfers between devices with their start and end apart: 2, of which 1 were waited for; matrix products, arithmetic and copies ran while one was open for 2% of the time, Pallas kernels for 0%

commit v1 on v0

v1 whole, which is shorter than its diff:
```python
import functools
import math

import jax
import jax.numpy as jnp
from jax import lax
from jax.experimental import pallas as pl
from jax.experimental.pallas import tpu as pltpu
from jax.sharding import PartitionSpec as P

LOG2E = 1.4426950408889634
LANE_ROWS = 16
DEPTH = 3
VMEM_BYTES = 48 * 1024 * 1024


def largest_block(rows, limit):
    units = rows // LANE_ROWS
    best = 1
    for size in range(1, units + 1):
        if units % size == 0 and size * LANE_ROWS <= limit:
            best = size
    return best * LANE_ROWS


def any_spec():
    return pl.BlockSpec(memory_space=pl.ANY)


def vmem_spec():
    return pl.BlockSpec(memory_space=pltpu.VMEM)


def smem_spec():
    return pl.BlockSpec(memory_space=pltpu.SMEM)


def prepare_kernel(counts_ref, valid_ref, temp_ref, owner_ref, out_ref):
    children, rows = counts_ref.shape
    slot = lax.broadcasted_iota(jnp.int32, (children, rows), 0)
    powered = jnp.exp(jnp.log(counts_ref[...].astype(jnp.float32)) * temp_ref[...])
    weights = jnp.where(slot < valid_ref[...], powered, 0.0)
    out_ref[:children, :] = weights / jnp.sum(weights, axis=0, keepdims=True)
    extra = out_ref.shape[0] - children
    out_ref[children:, :] = jnp.broadcast_to(owner_ref[...].astype(jnp.float32), (extra, rows))


def chunk_copies(x_hbm, x_ref, sems, chunk):
    def copy(index):
        window = pl.ds(index * chunk, chunk)
        return pltpu.make_async_copy(x_hbm.at[window, :], x_ref.at[window, :], sems.at[index])

    return copy


def stats_kernel(chunk, step, x_hbm, out_ref, x_ref, sems):
    total, lanes = x_ref.shape
    copy = chunk_copies(x_hbm, x_ref, sems, chunk)
    chunks = total // chunk
    for index in range(chunks):
        copy(index).start()

    def one(index, carry):
        top, acc = carry
        copy(index).wait()
        base = index * chunk

        def max_step(i, best):
            for s in range(step // LANE_ROWS):
                row = pl.multiple_of(base + i * step + s * LANE_ROWS, LANE_ROWS)
                best = jnp.maximum(best, x_ref[pl.ds(row, LANE_ROWS), :])
            return best

        new_top = lax.fori_loop(0, chunk // step, max_step, top)
        wide = new_top.astype(jnp.float32)
        acc = acc * jnp.exp2((top.astype(jnp.float32) - wide) * LOG2E)

        def sum_step(i, total_sum):
            for s in range(step // LANE_ROWS):
                row = pl.multiple_of(base + i * step + s * LANE_ROWS, LANE_ROWS)
                values = x_ref[pl.ds(row, LANE_ROWS), :].astype(jnp.float32)
                total_sum = total_sum + jnp.exp2((values - wide) * LOG2E)
            return total_sum

        acc = lax.fori_loop(0, chunk // step, sum_step, acc)
        return new_top, acc

    start = (
        jnp.full((LANE_ROWS, lanes), -3.0e38, jnp.bfloat16),
        jnp.zeros((LANE_ROWS, lanes), jnp.float32),
    )
    top, acc = lax.fori_loop(0, chunks, one, start)
    wide = top.astype(jnp.float32)
    row_top = jnp.max(wide, axis=0, keepdims=True)
    row_sum = jnp.sum(acc * jnp.exp2((wide - row_top) * LOG2E), axis=0, keepdims=True)
    out_ref[0:1, :] = row_top
    out_ref[1:2, :] = row_sum
    out_ref[2:, :] = jnp.zeros((out_ref.shape[0] - 2, lanes), jnp.float32)


def dense_rows(ids_ref, targets_ref, first_row, shape):
    row = lax.broadcasted_iota(jnp.int32, shape, 0) + first_row

    def add(j, dense):
        hit = ids_ref[pl.ds(j, 1), :] == row
        return dense + jnp.where(hit, targets_ref[pl.ds(j, 1), :], 0.0)

    return lax.fori_loop(0, ids_ref.shape[0], add, jnp.zeros(shape, jnp.float32))


def lists_kernel(
    blocks, bucket, group, place_ref, *refs
):
    routed = refs[:blocks]
    ids_ref, stats_ref, x_hbm = refs[blocks : blocks + 3]
    local_ref, targets_ref, index_ref, share_ref, value_ref, flag_ref, out_ref = refs[
        blocks + 3 : blocks + 10
    ]
    x_ref, over_ref, sems = refs[blocks + 10 :]
    total, lanes = x_ref.shape
    children = ids_ref.shape[0]
    buckets = total // bucket
    groups = buckets // group
    span = group * bucket
    slots = group * LANE_ROWS
    copy = chunk_copies(x_hbm, x_ref, sems, bucket)
    for index in range(buckets):
        copy(index).start()
    local = ids_ref[...] - place_ref[0]
    local_ref[...] = local

    position = lax.broadcasted_iota(jnp.int32, (lanes, lanes), 0) + place_ref[1]
    parts = jnp.zeros((3 * children, lanes), jnp.float32)
    for block in routed:
        owner = block[children : children + 1, :].astype(jnp.int32)
        matcher = jnp.where(owner == position, 1.0, 0.0).astype(jnp.bfloat16)
        rest = block[:children, :]
        pieces = []
        for _ in range(3):
            piece = rest.astype(jnp.bfloat16)
            pieces.append(piece)
            rest = rest - piece.astype(jnp.float32)
        stacked = jnp.concatenate(pieces, axis=0)
        parts = parts + lax.dot_general(
            stacked, matcher, (((1,), (1,)), ((), ())), preferred_element_type=jnp.float32
        )
    targets = parts[:children] + parts[children : 2 * children] + parts[2 * children :]
    targets_ref[...] = targets

    counts = []
    for g in range(groups):
        inside = (local >= g * span) & (local < (g + 1) * span)
        counts.append(
            jnp.max(jnp.sum(jnp.where(inside, 1.0, 0.0), axis=0, keepdims=True)).astype(jnp.int32)
        )

    big = jnp.int32(1 << 30)
    slot_row = lax.broadcasted_iota(jnp.int32, (slots, lanes), 0)
    slot_base = (slot_row // LANE_ROWS) * bucket + slot_row % LANE_ROWS
    for g in range(groups):

        def push(r, carry, g=g):
            last, index, share = carry
            here = local_ref[...]
            later = jnp.where((here > last) & (here < (g + 1) * span), here, big)
            found = jnp.min(later, axis=0, keepdims=True)
            amount = jnp.sum(
                jnp.where(here == found, targets_ref[...], 0.0), axis=0, keepdims=True
            )
            away = found - (g * span) - slot_base
            hit = (away >= 0) & (away < bucket) & ((away & (LANE_ROWS - 1)) == 0)
            at = (away // LANE_ROWS).astype(jnp.float32)
            new_index = [jnp.where(hit, at, index[0])]
            new_share = [jnp.where(hit, amount, share[0])]
            for k in range(1, DEPTH + 1):
                new_index.append(jnp.where(hit, index[k - 1], index[k]))
            for k in range(1, DEPTH):
                new_share.append(jnp.where(hit, share[k - 1], share[k]))
            return found, tuple(new_index), tuple(new_share)

        none = jnp.full((slots, lanes), -1.0, jnp.float32)
        zero = jnp.zeros((slots, lanes), jnp.float32)
        first = jnp.full((1, lanes), g * span - 1, jnp.int32)
        _, index, share = lax.fori_loop(
            0, counts[g], push, (first, (none,) * (DEPTH + 1), (zero,) * DEPTH)
        )
        for k in range(DEPTH):
            index_ref[k, g * slots : (g + 1) * slots, :] = index[k].astype(jnp.bfloat16)
            share_ref[k, g * slots : (g + 1) * slots, :] = share[k]
        over_ref[g] = jnp.max(index[DEPTH], axis=0, keepdims=True)
    for g in range(groups):
        flag_ref[g] = jnp.where(jnp.max(over_ref[g]) >= 0.0, 1, 0).astype(jnp.int32)

    out_ref[...] = stats_ref[...]

    def pick(b, picked):
        copy(b).wait()
        base = pl.multiple_of(b * bucket, LANE_ROWS)
        at = pl.ds(pl.multiple_of(b * LANE_ROWS, LANE_ROWS), LANE_ROWS)

        def fast():
            index = [index_ref[k, at, :] for k in range(DEPTH)]
            found = [jnp.zeros((LANE_ROWS, lanes), jnp.bfloat16)] * DEPTH
            for i in range(bucket // LANE_ROWS):
                values = x_ref[pl.ds(base + i * LANE_ROWS, LANE_ROWS), :]
                mark = jnp.bfloat16(i)
                found = [jnp.where(index[k] == mark, values, found[k]) for k in range(DEPTH)]
            extra = jnp.zeros((LANE_ROWS, lanes), jnp.float32)
            for k in range(DEPTH):
                value_ref[k, at, :] = found[k]
                extra = extra + share_ref[k, at, :] * found[k].astype(jnp.float32)
            return extra

        def slow():
            def add(i, extra):
                row = pl.multiple_of(base + i * LANE_ROWS, LANE_ROWS)
                dense = dense_rows(local_ref, targets_ref, row, (LANE_ROWS, lanes))
                values = x_ref[pl.ds(row, LANE_ROWS), :].astype(jnp.float32)
                return extra + jnp.where(dense != 0.0, dense * values, 0.0)

            zero = jnp.zeros((LANE_ROWS, lanes), jnp.float32)
            for k in range(DEPTH):
                value_ref[k, at, :] = zero.astype(jnp.bfloat16)
            return lax.fori_loop(0, bucket // LANE_ROWS, add, zero)

        return picked + lax.cond(flag_ref[b // group] == 0, fast, slow)

    picked = lax.fori_loop(0, buckets, pick, jnp.zeros((LANE_ROWS, lanes), jnp.float32))
    out_ref[2:3, :] = jnp.sum(picked, axis=0, keepdims=True)


def gradient_kernel(
    bucket,
    group,
    flag_ref,
    lse_ref,
    local_ref,
    targets_ref,
    index_ref,
    share_ref,
    value_ref,
    x_hbm,
    out_hbm,
    x_ref,
    out_ref,
    in_sems,
    out_sems,
):
    total, lanes = x_ref.shape
    buckets = total // bucket
    copy = chunk_copies(x_hbm, x_ref, in_sems, bucket)

    def back(index):
        window = pl.ds(index * bucket, bucket)
        return pltpu.make_async_copy(out_ref.at[window, :], out_hbm.at[window, :], out_sems.at[index])

    for index in range(buckets):
        copy(index).start()
    lse = jnp.broadcast_to(lse_ref[0:1, :], (LANE_ROWS, lanes))

    def one(b, carry):
        copy(b).wait()
        base = pl.multiple_of(b * bucket, LANE_ROWS)
        at = pl.ds(pl.multiple_of(b * LANE_ROWS, LANE_ROWS), LANE_ROWS)

        @pl.when(flag_ref[b // group] == 0)
        def _():
            index = [index_ref[k, at, :] for k in range(DEPTH)]
            given = []
            for k in range(DEPTH):
                value = value_ref[k, at, :].astype(jnp.float32)
                soft = jnp.exp2((value - lse) * LOG2E)
                given.append((soft - share_ref[k, at, :]).astype(jnp.bfloat16))
            for i in range(bucket // LANE_ROWS):
                row = pl.ds(base + i * LANE_ROWS, LANE_ROWS)
                values = x_ref[row, :].astype(jnp.float32)
                result = jnp.exp2((values - lse) * LOG2E).astype(jnp.bfloat16)
                mark = jnp.bfloat16(i)
                for k in range(DEPTH):
                    result = jnp.where(index[k] == mark, given[k], result)
                out_ref[row, :] = result

        @pl.when(flag_ref[b // group] != 0)
        def _():
            def fill(i, unused):
                first = pl.multiple_of(base + i * LANE_ROWS, LANE_ROWS)
                dense = dense_rows(local_ref, targets_ref, first, (LANE_ROWS, lanes))
                row = pl.ds(first, LANE_ROWS)
                values = x_ref[row, :].astype(jnp.float32)
                out_ref[row, :] = (jnp.exp2((values - lse) * LOG2E) - dense).astype(jnp.bfloat16)
                return unused

            lax.fori_loop(0, bucket // LANE_ROWS, fill, 0)

        back(b).start()
        return carry

    lax.fori_loop(0, buckets, one, 0)
    for index in range(buckets):
        back(index).wait()


def shifted(value, axis, size):
    result = []
    for shift in range(1, size):
        pairs = [(i, (i + shift) % size) for i in range(size)]
        result.append(lax.ppermute(value, axis, pairs))
    return result


def merge(one, other):
    top = jnp.maximum(one[0:1], other[0:1])
    total = one[1:2] * jnp.exp(one[0:1] - top) + other[1:2] * jnp.exp(other[0:1] - top)
    picked = one[2:3] + other[2:3]
    return jnp.concatenate([top, total, picked, jnp.zeros_like(one[3:])], axis=0)


def body(logits, child_ids, leaf_counts, leaf_valid, leaf_temp, leaf_owner):
    lanes, columns = logits.shape
    children = child_ids.shape[1]
    groups = lax.axis_size("dp")
    shards = lax.axis_size("tensor")
    f32 = jnp.float32
    params = pltpu.CompilerParams(vmem_limit_bytes=VMEM_BYTES)
    x = logits.T
    ids = child_ids.T
    place = jnp.stack([lax.axis_index("tensor") * columns, lax.axis_index("dp") * lanes])
    place = place.astype(jnp.int32)

    leaf = pl.pallas_call(
        prepare_kernel,
        out_shape=jax.ShapeDtypeStruct((children + 8, lanes), f32),
        name="prepare",
    )(
        leaf_counts.T,
        leaf_valid.reshape(1, lanes),
        leaf_temp.reshape(1, lanes),
        leaf_owner.reshape(1, lanes),
    )
    routed = [leaf] + shifted(leaf, "dp", groups)

    chunk = largest_block(columns, 2112)
    step = largest_block(chunk, 192)
    stats = pl.pallas_call(
        functools.partial(stats_kernel, chunk, step),
        out_shape=jax.ShapeDtypeStruct((8, lanes), f32),
        in_specs=[any_spec()],
        out_specs=vmem_spec(),
        scratch_shapes=[
            pltpu.VMEM((columns, lanes), jnp.bfloat16),
            pltpu.SemaphoreType.DMA((columns // chunk,)),
        ],
        compiler_params=params,
        name="stats",
    )(x)

    bucket = largest_block(columns, 704)
    buckets = columns // bucket
    group = 3 if buckets % 3 == 0 else 1
    listed = (DEPTH, buckets * LANE_ROWS, lanes)
    local, targets, index, share, value, flags, sums = pl.pallas_call(
        functools.partial(lists_kernel, groups, bucket, group),
        out_shape=(
            jax.ShapeDtypeStruct((children, lanes), jnp.int32),
            jax.ShapeDtypeStruct((children, lanes), f32),
            jax.ShapeDtypeStruct(listed, jnp.bfloat16),
            jax.ShapeDtypeStruct(listed, f32),
            jax.ShapeDtypeStruct(listed, jnp.bfloat16),
            jax.ShapeDtypeStruct((buckets // group,), jnp.int32),
            jax.ShapeDtypeStruct((8, lanes), f32),
        ),
        in_specs=[smem_spec()] + [vmem_spec()] * (groups + 2) + [any_spec()],
        out_specs=(vmem_spec(),) * 5 + (smem_spec(), vmem_spec()),
        scratch_shapes=[
            pltpu.VMEM((columns, lanes), jnp.bfloat16),
            pltpu.VMEM((buckets // group, 1, lanes), f32),
            pltpu.SemaphoreType.DMA((buckets,)),
        ],
        compiler_params=params,
        name="lists",
    )(place, *routed, ids, stats, x)

    hop = 1
    while hop < shards:
        pairs = [(i, i ^ hop) for i in range(shards)]
        sums = merge(sums, lax.ppermute(sums, "tensor", pairs))
        hop *= 2
    lse = sums[0:1] + jnp.log(sums[1:2])
    losses = lse - sums[2:3]
    row_loss = losses.reshape(lanes)
    own = jnp.broadcast_to(jnp.sum(losses), (8, 128))
    gathered = lax.all_gather(own[0:1, 0:1], "dp")
    mean_loss = jnp.sum(gathered) / (groups * lanes)

    gradient = pl.pallas_call(
        functools.partial(gradient_kernel, bucket, group),
        out_shape=jax.ShapeDtypeStruct((columns, lanes), jnp.bfloat16),
        in_specs=[smem_spec()] + [vmem_spec()] * 6 + [any_spec()],
        out_specs=any_spec(),
        scratch_shapes=[
            pltpu.VMEM((columns, lanes), jnp.bfloat16),
            pltpu.VMEM((columns, lanes), jnp.bfloat16),
            pltpu.SemaphoreType.DMA((buckets,)),
            pltpu.SemaphoreType.DMA((buckets,)),
        ],
        compiler_params=params,
        name="gradient",
    )(flags, lse, local, targets, index, share, value, x)
    return gradient.T, row_loss, mean_loss


def solution(mesh):
    return jax.shard_map(
        body,
        mesh=mesh,
        in_specs=(P("dp", "tensor"), P("dp", None), P("dp", None), P("dp"), P("dp"), P("dp")),
        out_specs=(P("dp", "tensor"), P("dp"), P()),
        check_vma=False,
    )
```

time: 427 us -> 59.3 us (0.14)
  other arithmetic: 368 us -> 2.03 us
  blocking collectives: 39.6 us -> 10 us
  Pallas kernels: 0 us -> 28.7 us
    reduce_sum x5 -> x2, other arithmetic: 343 us -> 1.79 us  [the longest x1 1.18 us: body(): own = jnp.broadcast_to(jnp.sum(losses), (8, 128))]
    pallas_call x0 -> x4, Pallas kernels: none -> 28.7 us  [the longest x1 11 us: body(): pl.pallas_call(functools.partial(lists_kernel, groups, bucket, group), ou...]
    psum x2 -> x0, blocking collectives: 24.3 us -> none  [the longest x1 13.6 us: body(): sumexp, picked = lax.psum((own_sum, picked_part), 'tensor')]
    pmax x1 -> x0, blocking collectives: 15.4 us -> none  [body(): row_top = lax.pmax(own_top_narrow, 'tensor').astype(jnp.float32)]
    convert_element_type x3 -> x0, other arithmetic: 15 us -> none  [the longest x1 15 us: body(): (jnp.exp(values - row_top[:, None]) * scale[:, None] - target_dense).asty...]
    unnamed x0 -> x1, blocking collectives: none -> 10 us
    ppermute x0 -> x6, starting transfers between devices: none -> 9.02 us  [the longest x3 5.02 us: shifted(): result.append(lax.ppermute(value, axis, pairs))]
    all_to_all x2 -> x0, starting transfers between devices: 8.48 us -> none  [the longest x1 5.19 us: body(): lax.all_to_all(labels, 'dp', split_axis=0, concat_axis=0, tiled=True)]
  transfers between devices with their start and end apart: 2 -> 6, of which waited for: 1 -> 3; matrix products, arithmetic and copies ran while one was open for 2% -> 1% of each run, Pallas kernels for 0% -> 13%
where the time goes in v1:
time: 59.3 us; the launch traced here: 59.1 us
  Pallas kernels  28.7 us (48%)
  blocking collectives  10 us (17%)
  starting transfers between devices  9.02 us (15%)
  waiting for transfers between devices  4.79 us (8%)
  between operations  2.5 us (4%)
  local copies, waits for them, and re-layouts  2.07 us (3%)
  other arithmetic  2.03 us (3%)
    pallas_call x1, Pallas kernels, body(): pl.pallas_call(functools.partial(lists_kernel, groups, bucket, group), ou...  11 us
    unnamed x1, blocking collectives  10 us
    pallas_call x1, Pallas kernels, body(): pl.pallas_call(functools.partial(gradient_kernel, bucket, group), out_sha...  8.66 us
    pallas_call x1, Pallas kernels, body(): pl.pallas_call(functools.partial(stats_kernel, chunk, step), out_shape=ja...  7.44 us
    ppermute x3, starting transfers between devices, shifted(): result.append(lax.ppermute(value, axis, pairs))  5.02 us
    ppermute x3, waiting for transfers between devices, body(): sums = merge(sums, lax.ppermute(sums, 'tensor', pairs))  4.78 us
    ppermute x3, starting transfers between devices, body(): sums = merge(sums, lax.ppermute(sums, 'tensor', pairs))  4 us
    unnamed x9, local copies, waits for them, and re-layouts  2 us
  transfers between devices with their start and end apart: 6, of which 3 were waited for; matrix products, arithmetic and copies ran while one was open for 1% of the time, Pallas kernels for 13%

profile of v1, /device:TPU:0, one launch (start us, length us, event | category | flops | bytes accessed | tf_op | source)
XLA Modules:
  0.0 59.1 jit_solution(2545141649771091224)
XLA Ops:
  0.6 0.0 copy-start.1
  0.6 1.6 %prepare.1.refs_0_ = f32[72,256]{1,0:T(8,128)} custom-call(s32[64,256]{1,0:T(8,128)} %bitcast.17, s32[1,256]{1,0:T(1,128)} %bitcast.18, f32[1,256]{1,0:T(1,128)} %bitcast.19, s32[1,256]{1,0:T(1,128)} %bitcast.20), custom_call_target="tpu_custom_call" | custom-call | tf_op jit(solution)/shard_map/prepare/pallas_call | solution.py:330
  2.2 0.0 copy-start
  2.2 3.9 %collective-permute-start.2 = (f32[72,256]{1,0:T(8,128)}, f32[72,256]{1,0:T(8,128)S(1)}, u32[]{:S(2)}, u32[]{:S(2)}) collective-permute-start(f32[72,256]{1,0:T(8,128)} %prepare.1.refs_0_), channel_id=1, source_target_pairs={{0,24},{8,0},{16,8},{24,16},{1,25},{9,1},{17,9},{25,17},{2,26},{10... | collective-permute-start | bytes 221192 | tf_op jit(solution)/shard_map/ppermute | solution.py:307
  6.1 0.5 collective-permute-start.1
  6.6 0.6 %collective-permute-start = (f32[72,256]{1,0:T(8,128)}, f32[72,256]{1,0:T(8,128)S(1)}, u32[]{:S(2)}, u32[]{:S(2)}) collective-permute-start(f32[72,256]{1,0:T(8,128)} %prepare.1.refs_0_), channel_id=1, source_target_pairs={{0,8},{8,16},{16,24},{24,0},{1,9},{9,17},{17,25},{25,1},{2,10},{10... | collective-permute-start | bytes 221192 | tf_op jit(solution)/shard_map/ppermute | solution.py:307
  7.2 0.0 copy-start.2
  7.2 7.4 %stats.1.refs_5_ = f32[8,256]{1,0:T(8,128)S(1)} custom-call(bf16[19008,256]{1,0:T(8,128)(2,1)} %bitcast.13), custom_call_target="tpu_custom_call" | custom-call | tf_op jit(solution)/shard_map/stats/pallas_call | solution.py:344
  14.7 0.1 pad_add_fusion.place_ref
  14.8 0.0 collective-permute-done.2.refs_3_
  14.8 0.0 collective-permute-done.1.refs_2_
  14.8 0.0 collective-permute-done.refs_1_
  14.8 0.0 copy-done.1
  14.8 0.0 copy-done
  14.8 11.0 %lists.1 = (s32[64,256]{1,0:T(8,128)S(1)}, f32[64,256]{1,0:T(8,128)S(1)}, bf16[3,432,256]{2,1,0:T(8,128)(2,1)S(1)}, f32[3,432,256]{2,1,0:T(8,128)S(1)}, bf16[3,4...) custom-call(s32[2]{0:T(128)S(1)} %pad_add_fusion.place_ref, f32[72,256]{1,0:T(8,128)S(1)} %copy-done, ...), custom_call_target="tpu_custom_call" | custom-call | tf_op jit(solution)/shard_map/lists/pallas_call | solution.py:361
  25.8 0.1 collective-permute-start.3
  25.9 0.1 pad.7.clone
  26.0 1.1 %collective-permute-done.3 = f32[8,256]{1,0:T(8,128)S(1)} collective-permute-done((f32[8,256]{1,0:T(8,128)S(1)}, f32[8,256]{1,0:T(8,128)S(1)}, u32[]{:S(2)}, u32[]{:S(2)}) %collective-permute-start.3) | collective-permute-done | bytes 8224 | tf_op jit(solution)/shard_map/ppermute | solution.py:386
  27.0 0.1 maximum_maximum_fusion
  27.1 1.5 %collective-permute-start.4 = (f32[8,256]{1,0:T(8,128)S(1)}, f32[8,256]{1,0:T(8,128)S(1)}, u32[]{:S(2)}, u32[]{:S(2)}) collective-permute-start(f32[8,256]{1,0:T(8,128)S(1)} %maximum_maximum_fusion), channel_id=1, source_target_pairs={{0,2},{1,3},{2,0},{3,1},{4,6},{5,7},{6,4},{7,5},{8,10},{9,11},{10,... | collective-permute-start | bytes 24584 | tf_op jit(solution)/shard_map/ppermute | solution.py:386
  28.6 2.2 %collective-permute-done.4 = f32[8,256]{1,0:T(8,128)S(1)} collective-permute-done((f32[8,256]{1,0:T(8,128)S(1)}, f32[8,256]{1,0:T(8,128)S(1)}, u32[]{:S(2)}, u32[]{:S(2)}) %collective-permute-start.4) | collective-permute-done | bytes 8224 | tf_op jit(solution)/shard_map/ppermute | solution.py:386
  30.8 0.1 maximum_maximum_fusion.1
  30.9 2.5 %collective-permute-start.5 = (f32[8,256]{1,0:T(8,128)S(1)}, f32[8,256]{1,0:T(8,128)S(1)}, u32[]{:S(2)}, u32[]{:S(2)}) collective-permute-start(f32[8,256]{1,0:T(8,128)S(1)} %maximum_maximum_fusion.1), channel_id=1, source_target_pairs={{0,4},{1,5},{2,6},{3,7},{4,0},{5,1},{6,2},{7,3},{8,12},{9,13},{10,... | collective-permute-start | bytes 24584 | tf_op jit(solution)/shard_map/ppermute | solution.py:386
  33.3 0.0 copy-done.2
  33.3 0.6 dynamic-slice
  33.9 1.5 %collective-permute-done.5 = f32[8,256]{1,0:T(8,128)S(1)} collective-permute-done((f32[8,256]{1,0:T(8,128)S(1)}, f32[8,256]{1,0:T(8,128)S(1)}, u32[]{:S(2)}, u32[]{:S(2)}) %collective-permute-start.5) | collective-permute-done | bytes 8224 | tf_op jit(solution)/shard_map/ppermute | solution.py:386
  35.4 1.2 %fusion.6 = (f32[]{:T(128)}, f32[1,256]{1,0:T(1,128)}, f32[1,256]{1,0:T(1,128)S(1)}) fusion(f32[1,256]{1,0:T(1,128)S(1)} %get-tuple-element.25, f32[8,256]{1,0:T(8,128)S(1)} %collective-permute-done.5, f32[1,256]{1,0:T(1,128)S(1)} %get-tuple-element.20, f32[1,256]{1,0:T(1,128)S(1)} %get-tuple-element.21), kind=kLoop, calls=%fused_computation.19 | loop fusion | flops 2559 | bytes 8196 | tf_op jit(solution)/shard_map/reduce_sum | solution.py:391
  36.6 1.4 %dynamic-update-slice = f32[4]{0:T(128)S(1)} dynamic-update-slice(f32[4]{0:T(128)S(1)} %broadcast.7, f32[1]{0:T(128)} %bitcast.10, u32[]{:T(128)} %bitcast.11) | dynamic-update-slice | bytes 12
  38.0 10.0 %all-reduce = f32[4]{0:T(128)S(1)} all-reduce(f32[4]{0:T(128)S(1)} %dynamic-update-slice), channel_id=1, replica_groups=mesh['dp'=4,'tensor'=8] {'dp'}, use_global_device_ids=true, to_apply=%add | all-reduce | flops 4 | bytes 32
  48.0 0.6 %reduce = f32[]{:T(128)} reduce(f32[4]{0:T(128)S(1)} %all-reduce, f32[]{:T(128)} %constant.16.clone.1), dimensions={0}, to_apply=%region_1.0 | reduce | flops 3 | bytes 24 | tf_op jit(solution)/shard_map/reduce_sum | solution.py:393
  49.3 8.7 %gradient.1 = bf16[19008,256]{1,0:T(8,128)(2,1)} custom-call(s32[9]{0:T(128)S(1)} %get-tuple-element.10.flag_ref, f32[1,256]{1,0:T(1,128)S(1)} %get-tuple-element.19.lse_ref, s32[64,256]{1,0:T(8,128)S(1)} %get-tuple-element.12.local_ref, f32[64,256]{1,0:T(8,128)S(1)} %get-tuple-element.13.targets_ref, bf16[3,432,256]{2,1,0:T(8,128)(2,1)S(1)} %get-tuple-element.14.index_ref, ...), custom_call_target="tpu_custom_call" | custom-call | tf_op jit(solution)/shard_map/gradient/pallas_call | solution.py:395
  (4 shorter events, 0.0 us)
Async XLA Ops:
  0.6 14.2 %copy-start.1 = (s32[256,64]{0,1:T(8,128)S(1)}, s32[256,64]{0,1:T(8,128)}, u32[]{:S(2)}) copy-start(s32[256,64]{0,1:T(8,128)} %param.7) | copy-start | bytes 196612
  2.2 12.6 %copy-start = (f32[72,256]{1,0:T(8,128)S(1)}, f32[72,256]{1,0:T(8,128)}, u32[]{:S(2)}) copy-start(f32[72,256]{1,0:T(8,128)} %prepare.1.refs_0_) | copy-start | bytes 221188
  2.2 12.6 %collective-permute-start.2 = (f32[72,256]{1,0:T(8,128)}, f32[72,256]{1,0:T(8,128)S(1)}, u32[]{:S(2)}, u32[]{:S(2)}) collective-permute-start(f32[72,256]{1,0:T(8,128)} %prepare.1.refs_0_), channel_id=1, source_target_pairs={{0,24},{8,0},{16,8},{24,16},{1,25},{9,1},{17,9},{25,17},{2,26},{10... | collective-permute-start | bytes 221192 | tf_op jit(solution)/shard_map/ppermute | solution.py:307
  6.1 8.6 %collective-permute-start.1 = (f32[72,256]{1,0:T(8,128)}, f32[72,256]{1,0:T(8,128)S(1)}, u32[]{:S(2)}, u32[]{:S(2)}) collective-permute-start(f32[72,256]{1,0:T(8,128)} %prepare.1.refs_0_), channel_id=1, source_target_pairs={{0,16},{8,24},{16,0},{24,8},{1,17},{9,25},{17,1},{25,9},{2,18},{10... | collective-permute-start | bytes 221192 | tf_op jit(solution)/shard_map/ppermute | solution.py:307
  6.6 8.1 %collective-permute-start = (f32[72,256]{1,0:T(8,128)}, f32[72,256]{1,0:T(8,128)S(1)}, u32[]{:S(2)}, u32[]{:S(2)}) collective-permute-start(f32[72,256]{1,0:T(8,128)} %prepare.1.refs_0_), channel_id=1, source_target_pairs={{0,8},{8,16},{16,24},{24,0},{1,9},{9,17},{17,25},{25,1},{2,10},{10... | collective-permute-start | bytes 221192 | tf_op jit(solution)/shard_map/ppermute | solution.py:307
  7.2 26.1 %copy-start.2 = (u32[32]{0:T(128)S(1)}, u32[32]{0:T(128)}, u32[]{:S(2)}) copy-start(u32[32]{0:T(128)} %constant.20) | copy-start | bytes 388
  25.8 1.2 %collective-permute-start.3 = (f32[8,256]{1,0:T(8,128)S(1)}, f32[8,256]{1,0:T(8,128)S(1)}, u32[]{:S(2)}, u32[]{:S(2)}) collective-permute-start(f32[8,256]{1,0:T(8,128)S(1)} %get-tuple-element.11), channel_id=1, source_target_pairs={{0,1},{1,0},{2,3},{3,2},{4,5},{5,4},{6,7},{7,6},{8,9},{9,8},{10,11... | collective-permute-start | bytes 24584 | tf_op jit(solution)/shard_map/ppermute | solution.py:386
  27.1 3.7 %collective-permute-start.4 = (f32[8,256]{1,0:T(8,128)S(1)}, f32[8,256]{1,0:T(8,128)S(1)}, u32[]{:S(2)}, u32[]{:S(2)}) collective-permute-start(f32[8,256]{1,0:T(8,128)S(1)} %maximum_maximum_fusion), channel_id=1, source_target_pairs={{0,2},{1,3},{2,0},{3,1},{4,6},{5,7},{6,4},{7,5},{8,10},{9,11},{10,... | collective-permute-start | bytes 24584 | tf_op jit(solution)/shard_map/ppermute | solution.py:386
  30.9 4.6 %collective-permute-start.5 = (f32[8,256]{1,0:T(8,128)S(1)}, f32[8,256]{1,0:T(8,128)S(1)}, u32[]{:S(2)}, u32[]{:S(2)}) collective-permute-start(f32[8,256]{1,0:T(8,128)S(1)} %maximum_maximum_fusion.1), channel_id=1, source_target_pairs={{0,4},{1,5},{2,6},{3,7},{4,0},{5,1},{6,2},{7,3},{8,12},{9,13},{10,... | collective-permute-start | bytes 24584 | tf_op jit(solution)/shard_map/ppermute | solution.py:386

commit v2 on v1

v2 whole, which is shorter than its diff:
```python
import functools
import math

import jax
import jax.numpy as jnp
from jax import lax
from jax.experimental import pallas as pl
from jax.experimental.pallas import tpu as pltpu
from jax.sharding import PartitionSpec as P

LOG2E = 1.4426950408889634
LANE_ROWS = 16
DEPTH = 3
UNROLL = 4
VMEM_BYTES = 32 * 1024 * 1024


def largest_block(rows, limit):
    units = rows // LANE_ROWS
    best = 1
    for size in range(1, units + 1):
        if units % size == 0 and size * LANE_ROWS <= limit:
            best = size
    return best * LANE_ROWS


def any_spec():
    return pl.BlockSpec(memory_space=pltpu.HBM)


def vmem_spec():
    return pl.BlockSpec(memory_space=pltpu.VMEM)


def smem_spec():
    return pl.BlockSpec(memory_space=pltpu.SMEM)


def prepare_kernel(counts_ref, valid_ref, temp_ref, owner_ref, out_ref):
    children, rows = counts_ref.shape
    slot = lax.broadcasted_iota(jnp.int32, (children, rows), 0)
    powered = jnp.exp(jnp.log(counts_ref[...].astype(jnp.float32)) * temp_ref[...])
    weights = jnp.where(slot < valid_ref[...], powered, 0.0)
    out_ref[:children, :] = weights / jnp.sum(weights, axis=0, keepdims=True)
    extra = out_ref.shape[0] - children
    out_ref[children:, :] = jnp.broadcast_to(owner_ref[...].astype(jnp.float32), (extra, rows))


def stats_kernel(block, x_hbm, out_ref, x_ref, sems):
    total, lanes = x_ref.shape
    blocks = total // block
    units = block // LANE_ROWS

    def copy(index):
        window = pl.ds(index * block, block)
        return pltpu.make_async_copy(x_hbm.at[window, :], x_ref.at[window, :], sems.at[index])

    for index in range(blocks):
        copy(index).start()

    def block_top(index, best):
        base = pl.multiple_of(index * block, LANE_ROWS)
        for i in range(units):
            best = jnp.maximum(best, x_ref[pl.ds(base + i * LANE_ROWS, LANE_ROWS), :])
        return best

    def block_sum(index, wide, acc):
        base = pl.multiple_of(index * block, LANE_ROWS)
        for i in range(units):
            values = x_ref[pl.ds(base + i * LANE_ROWS, LANE_ROWS), :].astype(jnp.float32)
            acc = acc + jnp.exp2((values - wide) * LOG2E)
        return acc

    def one(index, carry):
        top, acc = carry
        copy(index + 1).wait()
        new_top = block_top(index + 1, top)
        wide = top.astype(jnp.float32)
        acc = block_sum(index, wide, acc)
        acc = acc * jnp.exp2((wide - new_top.astype(jnp.float32)) * LOG2E)
        return new_top, acc

    copy(0).wait()
    top = block_top(0, jnp.full((LANE_ROWS, lanes), -3.0e38, jnp.bfloat16))
    top, acc = lax.fori_loop(0, blocks - 1, one, (top, jnp.zeros((LANE_ROWS, lanes), jnp.float32)))
    wide = top.astype(jnp.float32)
    acc = block_sum(blocks - 1, wide, acc)
    row_top = jnp.max(wide, axis=0, keepdims=True)
    row_sum = jnp.sum(acc * jnp.exp2((wide - row_top) * LOG2E), axis=0, keepdims=True)
    out_ref[0:1, :] = row_top
    out_ref[1:2, :] = row_sum
    out_ref[2:, :] = jnp.zeros((out_ref.shape[0] - 2, lanes), jnp.float32)


def dense_rows(ids_ref, targets_ref, first_row, shape):
    row = lax.broadcasted_iota(jnp.int32, shape, 0) + first_row

    def add(j, dense):
        hit = ids_ref[pl.ds(j, 1), :] == row
        return dense + jnp.where(hit, targets_ref[pl.ds(j, 1), :], 0.0)

    return lax.fori_loop(0, ids_ref.shape[0], add, jnp.zeros(shape, jnp.float32))


def lists_kernel(leaf_blocks, bucket, group, *refs):
    routed = refs[:leaf_blocks]
    ids_ref, stats_ref, x_ref = refs[leaf_blocks : leaf_blocks + 3]
    local_ref, targets_ref, index_ref, share_ref, value_ref, flag_ref, out_ref = refs[
        leaf_blocks + 3 : leaf_blocks + 10
    ]
    code_ref, rank_ref, slot_ref, at_ref, part_ref = refs[leaf_blocks + 10 :]
    f32 = jnp.float32
    total, lanes = x_ref.shape
    children = ids_ref.shape[0]
    buckets = total // bucket
    groups = buckets // group
    units = bucket // LANE_ROWS
    slots = group * LANE_ROWS
    local = ids_ref[...] - lax.axis_index("tensor") * total
    local_ref[...] = local

    inside = (local >= 0) & (local < total)
    unit = local // LANE_ROWS
    at_bucket = ((unit.astype(f32) + 0.5) * (1.0 / units)).astype(jnp.int32)
    at = unit - at_bucket * units
    slot = at_bucket * LANE_ROWS + (local & (LANE_ROWS - 1))
    slot = jnp.where(inside, slot, -1)
    slot_ref[:children, :] = slot
    code_ref[...] = slot * 256 + at + 1

    tiles = children // 8
    sublane = lax.broadcasted_iota(jnp.int32, (8, lanes), 0)
    tile_slot = [slot[8 * t : 8 * t + 8] for t in range(tiles)]
    depth = [jnp.zeros((8, lanes), jnp.int32) for _ in range(tiles)]
    for j in range(children):
        row = slot_ref[j : j + 1, :]
        own = j // 8
        hit = (tile_slot[own] == row) & (sublane > j % 8)
        depth[own] = depth[own] + jnp.where(hit, 1, 0)
        for t in range(own + 1, tiles):
            depth[t] = depth[t] + jnp.where(tile_slot[t] == row, 1, 0)
    depth = jnp.where(inside, jnp.concatenate(depth, axis=0), -1)

    lower = lax.broadcasted_iota(jnp.int32, (children, children), 0)
    lower = lower > lax.broadcasted_iota(jnp.int32, (children, children), 1)
    lower = jnp.where(lower, 1.0, 0.0).astype(jnp.bfloat16)
    counts = []
    for k in range(DEPTH):
        chosen = jnp.where(depth == k, 1.0, 0.0)
        rank = jnp.dot(lower, chosen.astype(jnp.bfloat16), preferred_element_type=f32)
        rank_ref[k] = jnp.where(depth == k, rank, -1.0)
        counts.append(jnp.max(jnp.sum(chosen, axis=0, keepdims=True)).astype(jnp.int32))
    deepest = jnp.max(depth.astype(f32)).astype(jnp.int32)

    position = lax.broadcasted_iota(jnp.int32, (lanes, lanes), 0) + lax.axis_index("dp") * lanes
    parts = jnp.zeros((3 * children, lanes), f32)
    for block in routed:
        owner = block[children : children + 1, :].astype(jnp.int32)
        matcher = jnp.where(owner == position, 1.0, 0.0).astype(jnp.bfloat16)
        rest = block[:children, :]
        pieces = []
        for _ in range(3):
            piece = rest.astype(jnp.bfloat16)
            pieces.append(piece)
            rest = rest - piece.astype(f32)
        stacked = jnp.concatenate(pieces, axis=0)
        parts = parts + lax.dot_general(
            stacked, matcher, (((1,), (1,)), ((), ())), preferred_element_type=f32
        )
    targets_ref[...] = parts[:children] + parts[children : 2 * children] + parts[2 * children :]

    for g in range(groups):
        flag_ref[g] = 0

    @pl.when(deepest >= DEPTH)
    def _():
        for g in range(groups):
            over = (depth >= DEPTH) & (slot >= g * slots) & (slot < (g + 1) * slots)
            flag_ref[g] = jnp.max(jnp.where(over, 1.0, 0.0)).astype(jnp.int32)

    steps = [(count + UNROLL - 1) // UNROLL for count in counts]
    for k in range(DEPTH):

        def compact(step, unused, k=k):
            for u in range(UNROLL):
                r = step * UNROLL + u
                hit = rank_ref[k] == r.astype(f32)
                code = jnp.sum(jnp.where(hit, code_ref[...], 0), axis=0, keepdims=True) - 1
                part = jnp.sum(jnp.where(hit, targets_ref[...], 0.0), axis=0, keepdims=True)
                row = pl.ds(k * children + r, 1)
                slot_ref[row, :] = code >> 8
                at_ref[row, :] = (code & 255).astype(f32)
                part_ref[row, :] = part
            return unused

        lax.fori_loop(0, steps[k], compact, 0)

    def fill(g, unused):
        slot_row = lax.broadcasted_iota(jnp.int32, (slots, lanes), 0) + g * slots
        index, share = [], []
        for k in range(DEPTH):

            def add(step, carry, k=k):
                found, amount = carry
                for u in range(UNROLL):
                    row = pl.ds(k * children + step * UNROLL + u, 1)
                    hit = slot_ref[row, :] == slot_row
                    found = jnp.where(hit, at_ref[row, :], found)
                    amount = jnp.where(hit, part_ref[row, :], amount)
                return found, amount

            none = jnp.full((slots, lanes), -1.0, f32)
            zero = jnp.zeros((slots, lanes), f32)
            found, amount = lax.fori_loop(0, steps[k], add, (none, zero))
            for earlier in range(k):
                same = index[earlier] == found
                share[earlier] = share[earlier] + jnp.where(same, amount, 0.0)
                found = jnp.where(same, -1.0, found)
                amount = jnp.where(same, 0.0, amount)
            index.append(found)
            share.append(amount)
        rows = pl.ds(pl.multiple_of(g * slots, LANE_ROWS), slots)
        for k in range(DEPTH):
            index_ref[k, rows, :] = index[k].astype(jnp.bfloat16)
            share_ref[k, rows, :] = share[k]
        return unused

    lax.fori_loop(0, groups, fill, 0)
    out_ref[...] = stats_ref[...]

    def pick(b, picked):
        base = pl.multiple_of(b * bucket, LANE_ROWS)
        at_rows = pl.ds(pl.multiple_of(b * LANE_ROWS, LANE_ROWS), LANE_ROWS)

        def fast():
            index = [index_ref[k, at_rows, :] for k in range(DEPTH)]
            found = [jnp.zeros((LANE_ROWS, lanes), jnp.bfloat16)] * DEPTH
            for i in range(units):
                values = x_ref[pl.ds(base + i * LANE_ROWS, LANE_ROWS), :]
                mark = jnp.bfloat16(i)
                found = [jnp.where(index[k] == mark, values, found[k]) for k in range(DEPTH)]
            extra = jnp.zeros((LANE_ROWS, lanes), f32)
            for k in range(DEPTH):
                value_ref[k, at_rows, :] = found[k]
                extra = extra + share_ref[k, at_rows, :] * found[k].astype(f32)
            return extra

        def slow():
            def add(i, extra):
                row = pl.multiple_of(base + i * LANE_ROWS, LANE_ROWS)
                dense = dense_rows(local_ref, targets_ref, row, (LANE_ROWS, lanes))
                values = x_ref[pl.ds(row, LANE_ROWS), :].astype(f32)
                return extra + dense * values

            zero = jnp.zeros((LANE_ROWS, lanes), f32)
            for k in range(DEPTH):
                value_ref[k, at_rows, :] = zero.astype(jnp.bfloat16)
            return lax.fori_loop(0, units, add, zero)

        return picked + lax.cond(flag_ref[b // group] == 0, fast, slow)

    picked = lax.fori_loop(0, buckets, pick, jnp.zeros((LANE_ROWS, lanes), f32))
    out_ref[2:3, :] = jnp.sum(picked, axis=0, keepdims=True)


def gradient_kernel(
    bucket,
    group,
    flag_ref,
    lse_ref,
    own_ref,
    local_ref,
    targets_ref,
    index_ref,
    share_ref,
    value_ref,
    x_ref,
    out_hbm,
    loss_ref,
    out_ref,
    sems,
):
    total, lanes = x_ref.shape
    buckets = total // bucket

    def back(index):
        window = pl.ds(index * bucket, bucket)
        return pltpu.make_async_copy(out_ref.at[window, :], out_hbm.at[window, :], sems.at[index])

    loss_ref[...] = own_ref[...]
    lse = jnp.broadcast_to(lse_ref[0:1, :], (LANE_ROWS, lanes))

    def one(b, carry):
        base = pl.multiple_of(b * bucket, LANE_ROWS)
        at = pl.ds(pl.multiple_of(b * LANE_ROWS, LANE_ROWS), LANE_ROWS)

        @pl.when(flag_ref[b // group] == 0)
        def _():
            index = [index_ref[k, at, :] for k in range(DEPTH)]
            given = []
            for k in range(DEPTH):
                value = value_ref[k, at, :].astype(jnp.float32)
                soft = jnp.exp2((value - lse) * LOG2E)
                given.append((soft - share_ref[k, at, :]).astype(jnp.bfloat16))
            for i in range(bucket // LANE_ROWS):
                row = pl.ds(base + i * LANE_ROWS, LANE_ROWS)
                values = x_ref[row, :].astype(jnp.float32)
                result = jnp.exp2((values - lse) * LOG2E).astype(jnp.bfloat16)
                mark = jnp.bfloat16(i)
                for k in range(DEPTH):
                    result = jnp.where(index[k] == mark, given[k], result)
                out_ref[row, :] = result

        @pl.when(flag_ref[b // group] != 0)
        def _():
            def fill(i, unused):
                first = pl.multiple_of(base + i * LANE_ROWS, LANE_ROWS)
                dense = dense_rows(local_ref, targets_ref, first, (LANE_ROWS, lanes))
                row = pl.ds(first, LANE_ROWS)
                values = x_ref[row, :].astype(jnp.float32)
                out_ref[row, :] = (jnp.exp2((values - lse) * LOG2E) - dense).astype(jnp.bfloat16)
                return unused

            lax.fori_loop(0, bucket // LANE_ROWS, fill, 0)

        back(b).start()
        return carry

    lax.fori_loop(0, buckets, one, 0)
    for index in range(buckets):
        back(index).wait()


def shifted(value, axis, size):
    result = []
    for shift in range(1, size):
        pairs = [(i, i ^ shift) for i in range(size)]
        result.append(lax.ppermute(value, axis, pairs))
    return result


def merge(one, other):
    top = jnp.maximum(one[0:1], other[0:1])
    total = one[1:2] * jnp.exp(one[0:1] - top) + other[1:2] * jnp.exp(other[0:1] - top)
    picked = one[2:3] + other[2:3]
    return jnp.concatenate([top, total, picked, jnp.zeros_like(one[3:])], axis=0)


def body(logits, child_ids, leaf_counts, leaf_valid, leaf_temp, leaf_owner):
    lanes, columns = logits.shape
    children = child_ids.shape[1]
    groups = lax.axis_size("dp")
    shards = lax.axis_size("tensor")
    f32 = jnp.float32
    params = pltpu.CompilerParams(vmem_limit_bytes=VMEM_BYTES)
    ids = child_ids.T

    leaf = pl.pallas_call(
        prepare_kernel,
        out_shape=jax.ShapeDtypeStruct((children + 8, lanes), f32),
        name="prepare",
    )(
        leaf_counts.T,
        leaf_valid.reshape(1, lanes),
        leaf_temp.reshape(1, lanes),
        leaf_owner.reshape(1, lanes),
    )
    routed = [leaf] + shifted(leaf, "dp", groups)

    bucket = largest_block(columns, 704)
    buckets = columns // bucket
    group = 3 if buckets % 3 == 0 else 1
    stats, x = pl.pallas_call(
        functools.partial(stats_kernel, bucket),
        out_shape=(
            jax.ShapeDtypeStruct((8, lanes), f32),
            jax.ShapeDtypeStruct((columns, lanes), jnp.bfloat16),
        ),
        in_specs=[any_spec()],
        out_specs=(vmem_spec(), vmem_spec()),
        scratch_shapes=[pltpu.SemaphoreType.DMA((buckets,))],
        compiler_params=params,
        name="stats",
    )(pltpu.with_memory_space_constraint(logits.T, pltpu.HBM))

    listed = (DEPTH, buckets * LANE_ROWS, lanes)
    compact = DEPTH * children + 8
    local, targets, index, share, value, flags, sums = pl.pallas_call(
        functools.partial(lists_kernel, groups, bucket, group),
        out_shape=(
            jax.ShapeDtypeStruct((children, lanes), jnp.int32),
            jax.ShapeDtypeStruct((children, lanes), f32),
            jax.ShapeDtypeStruct(listed, jnp.bfloat16),
            jax.ShapeDtypeStruct(listed, f32),
            jax.ShapeDtypeStruct(listed, jnp.bfloat16),
            jax.ShapeDtypeStruct((buckets // group,), jnp.int32),
            jax.ShapeDtypeStruct((8, lanes), f32),
        ),
        in_specs=[vmem_spec()] * (groups + 3),
        out_specs=(vmem_spec(),) * 5 + (smem_spec(), vmem_spec()),
        scratch_shapes=[
            pltpu.VMEM((children, lanes), jnp.int32),
            pltpu.VMEM((DEPTH, children, lanes), f32),
            pltpu.VMEM((compact, lanes), jnp.int32),
            pltpu.VMEM((compact, lanes), f32),
            pltpu.VMEM((compact, lanes), f32),
        ],
        compiler_params=params,
        name="lists",
    )(*routed, ids, stats, x)

    hop = 1
    while hop < shards:
        pairs = [(i, i ^ hop) for i in range(shards)]
        sums = merge(sums, lax.ppermute(sums, "tensor", pairs))
        hop *= 2
    lse = sums[0:1] + jnp.log(sums[1:2])
    own = lse - sums[2:3]
    others = shifted(own, "dp", groups)

    gradient, row_loss = pl.pallas_call(
        functools.partial(gradient_kernel, bucket, group),
        out_shape=(
            jax.ShapeDtypeStruct((columns, lanes), jnp.bfloat16),
            jax.ShapeDtypeStruct((1, lanes), f32),
        ),
        in_specs=[smem_spec()] + [vmem_spec()] * 8,
        out_specs=(any_spec(), vmem_spec()),
        scratch_shapes=[
            pltpu.VMEM((columns, lanes), jnp.bfloat16),
            pltpu.SemaphoreType.DMA((buckets,)),
        ],
        compiler_params=params,
        name="gradient",
    )(flags, lse, own, local, targets, index, share, value, x)
    losses = [own] + others
    while len(losses) > 1:
        losses = [losses[i] + losses[i + 1] for i in range(0, len(losses), 2)]
    mean_loss = jnp.sum(losses[0]) / (groups * lanes)
    return gradient.T, row_loss.reshape(lanes), mean_loss


def solution(mesh):
    return jax.shard_map(
        body,
        mesh=mesh,
        in_specs=(P("dp", "tensor"), P("dp", None), P("dp", None), P("dp"), P("dp"), P("dp")),
        out_specs=(P("dp", "tensor"), P("dp"), P()),
        check_vma=False,
    )
```

time: 59.3 us -> 43.8 us (0.74)
  blocking collectives: 10 us -> 0 us
  Pallas kernels: 28.7 us -> 22.6 us
  starting transfers between devices: 9.02 us -> 13 us
  local copies, waits for them, and re-layouts: 2.07 us -> 0.09 us
  other arithmetic: 2.03 us -> 0.79 us
    unnamed x1 -> x0, blocking collectives: 10 us -> none
    pallas_call x1, Pallas kernels: 11 us -> 7.07 us  [body(): pl.pallas_call(functools.partial(lists_kernel, groups, bucket, group), ou...]
    ppermute x3 -> x6, starting transfers between devices: 5.02 us -> 8.14 us  [shifted(): result.append(lax.ppermute(value, axis, pairs))]
    unnamed x9 -> x4, local copies, waits for them, and re-layouts: 2 us -> 0.01 us
    pallas_call x1, Pallas kernels: 7.44 us -> 6.02 us  [body(): pl.pallas_call(functools.partial(stats_kernel, bucket), out_shape=(jax.Sh...]
    reduce_sum x2 -> x1, other arithmetic: 1.79 us -> 0.6 us  [body(): mean_loss = jnp.sum(losses[0]) / (groups * lanes)]
    ppermute x3, starting transfers between devices: 4 us -> 4.88 us  [body(): sums = merge(sums, lax.ppermute(sums, 'tensor', pairs))]
    pallas_call x1, Pallas kernels: 8.66 us -> 8 us  [body(): pl.pallas_call(functools.partial(gradient_kernel, bucket, group), out_sha...]
  transfers between devices with their start and end apart: 6 -> 9, of which waited for: 3 -> 3; matrix products, arithmetic and copies ran while one was open for 1% -> 0% of each run, Pallas kernels for 13% -> 32%
where the time goes in v2:
time: 43.8 us; the launch traced here: 43.6 us
  Pallas kernels  22.6 us (52%)
  starting transfers between devices  13 us (30%)
  waiting for transfers between devices  4.53 us (10%)
  between operations  2.53 us (6%)
  other arithmetic  0.79 us (2%)
    ppermute x6, starting transfers between devices, shifted(): result.append(lax.ppermute(value, axis, pairs))  8.14 us
    pallas_call x1, Pallas kernels, body(): pl.pallas_call(functools.partial(gradient_kernel, bucket, group), out_sha...  8 us
    pallas_call x1, Pallas kernels, body(): pl.pallas_call(functools.partial(lists_kernel, groups, bucket, group), ou...  7.07 us
    pallas_call x1, Pallas kernels, body(): pl.pallas_call(functools.partial(stats_kernel, bucket), out_shape=(jax.Sh...  6.02 us
    ppermute x3, starting transfers between devices, body(): sums = merge(sums, lax.ppermute(sums, 'tensor', pairs))  4.88 us
    ppermute x3, waiting for transfers between devices, body(): sums = merge(sums, lax.ppermute(sums, 'tensor', pairs))  4.52 us
    pallas_call x1, Pallas kernels, body(): pl.pallas_call(prepare_kernel, out_shape=jax.ShapeDtypeStruct((children +...  1.57 us
  transfers between devices with their start and end apart: 9, of which 3 were waited for; matrix products, arithmetic and copies ran while one was open for 0% of the time, Pallas kernels for 32%

profile of v2, /device:TPU:0, one launch (start us, length us, event | category | flops | bytes accessed | tf_op | source)
XLA Modules:
  0.0 43.6 jit_solution(16749698084418372608)
XLA Ops:
  0.6 0.0 copy-start.1
  0.6 1.6 %prepare.1.refs_0_ = f32[72,256]{1,0:T(8,128)} custom-call(s32[64,256]{1,0:T(8,128)} %bitcast.10, s32[1,256]{1,0:T(1,128)} %bitcast.11, f32[1,256]{1,0:T(1,128)} %bitcast.12, s32[1,256]{1,0:T(1,128)} %bitcast.13), custom_call_target="tpu_custom_call" | custom-call | tf_op jit(solution)/shard_map/prepare/pallas_call | solution.py:358
  2.2 0.0 copy-start
  2.2 3.9 %collective-permute-start.2 = (f32[72,256]{1,0:T(8,128)}, f32[72,256]{1,0:T(8,128)S(1)}, u32[]{:S(2)}, u32[]{:S(2)}) collective-permute-start(f32[72,256]{1,0:T(8,128)} %prepare.1.refs_0_), channel_id=1, source_target_pairs={{0,24},{8,16},{16,8},{24,0},{1,25},{9,17},{17,9},{25,1},{2,26},{10... | collective-permute-start | bytes 221192 | tf_op jit(solution)/shard_map/ppermute | solution.py:338
  6.1 0.5 %collective-permute-start.1 = (f32[72,256]{1,0:T(8,128)}, f32[72,256]{1,0:T(8,128)S(1)}, u32[]{:S(2)}, u32[]{:S(2)}) collective-permute-start(f32[72,256]{1,0:T(8,128)} %prepare.1.refs_0_), channel_id=1, source_target_pairs={{0,16},{8,24},{16,0},{24,8},{1,17},{9,25},{17,1},{25,9},{2,18},{10... | collective-permute-start | bytes 221192 | tf_op jit(solution)/shard_map/ppermute | solution.py:338
  6.6 0.1 collective-permute-start
  6.7 6.0 %stats.1 = (f32[8,256]{1,0:T(8,128)S(1)}, bf16[19008,256]{1,0:T(8,128)(2,1)S(1)}) custom-call(bf16[19008,256]{1,0:T(8,128)(2,1)} %bitcast.9), custom_call_target="tpu_custom_call" | custom-call | tf_op jit(solution)/shard_map/stats/pallas_call | solution.py:373
  12.7 0.0 collective-permute-done.2.refs_3_
  12.7 0.0 collective-permute-done.1.refs_2_
  12.7 0.0 collective-permute-done.refs_1_
  12.8 0.0 copy-done.1
  12.8 0.0 copy-done
  12.8 7.1 %lists.1 = (s32[64,256]{1,0:T(8,128)S(1)}, f32[64,256]{1,0:T(8,128)S(1)}, bf16[3,432,256]{2,1,0:T(8,128)(2,1)S(1)}, f32[3,432,256]{2,1,0:T(8,128)S(1)}, bf16[3,4...) custom-call(f32[72,256]{1,0:T(8,128)S(1)} %copy-done, f32[72,256]{1,0:T(8,128)S(1)} %collective-permute-done.refs_1_, ...), custom_call_target="tpu_custom_call" | custom-call | tf_op jit(solution)/shard_map/lists/pallas_call | solution.py:388
  19.9 0.1 collective-permute-start.3
  19.9 0.1 pad.7.clone
  20.0 1.1 %collective-permute-done.3 = f32[8,256]{1,0:T(8,128)S(1)} collective-permute-done((f32[8,256]{1,0:T(8,128)S(1)}, f32[8,256]{1,0:T(8,128)S(1)}, u32[]{:S(2)}, u32[]{:S(2)}) %collective-permute-start.3) | collective-permute-done | bytes 8224 | tf_op jit(solution)/shard_map/ppermute | solution.py:415
  21.1 0.1 maximum_maximum_fusion
  21.2 2.1 %collective-permute-start.4 = (f32[8,256]{1,0:T(8,128)S(1)}, f32[8,256]{1,0:T(8,128)S(1)}, u32[]{:S(2)}, u32[]{:S(2)}) collective-permute-start(f32[8,256]{1,0:T(8,128)S(1)} %maximum_maximum_fusion), channel_id=1, source_target_pairs={{0,2},{1,3},{2,0},{3,1},{4,6},{5,7},{6,4},{7,5},{8,10},{9,11},{10,... | collective-permute-start | bytes 24584 | tf_op jit(solution)/shard_map/ppermute | solution.py:415
  23.2 1.6 %collective-permute-done.4 = f32[8,256]{1,0:T(8,128)S(1)} collective-permute-done((f32[8,256]{1,0:T(8,128)S(1)}, f32[8,256]{1,0:T(8,128)S(1)}, u32[]{:S(2)}, u32[]{:S(2)}) %collective-permute-start.4) | collective-permute-done | bytes 8224 | tf_op jit(solution)/shard_map/ppermute | solution.py:415
  24.9 0.1 maximum_maximum_fusion.1
  25.0 2.7 %collective-permute-start.5 = (f32[8,256]{1,0:T(8,128)S(1)}, f32[8,256]{1,0:T(8,128)S(1)}, u32[]{:S(2)}, u32[]{:S(2)}) collective-permute-start(f32[8,256]{1,0:T(8,128)S(1)} %maximum_maximum_fusion.1), channel_id=1, source_target_pairs={{0,4},{1,5},{2,6},{3,7},{4,0},{5,1},{6,2},{7,3},{8,12},{9,13},{10,... | collective-permute-start | bytes 24584 | tf_op jit(solution)/shard_map/ppermute | solution.py:415
  27.7 1.8 %collective-permute-done.5 = f32[8,256]{1,0:T(8,128)S(1)} collective-permute-done((f32[8,256]{1,0:T(8,128)S(1)}, f32[8,256]{1,0:T(8,128)S(1)}, u32[]{:S(2)}, u32[]{:S(2)}) %collective-permute-start.5) | collective-permute-done | bytes 8224 | tf_op jit(solution)/shard_map/ppermute | solution.py:415
  29.5 3.0 %collective-permute-start.8 = (f32[1,256]{1,0:T(1,128)S(1)}, f32[1,256]{1,0:T(1,128)S(1)}, u32[]{:S(2)}, u32[]{:S(2)}) collective-permute-start(f32[1,256]{1,0:T(1,128)S(1)} %get-tuple-element.25.own_ref), channel_id=1, source_target_pairs={{0,24},{8,16},{16,8},{24,0},{1,25},{9,17},{17,9},{25,1},{2,26},{10... | collective-permute-start | bytes 3080 | tf_op jit(solution)/shard_map/ppermute | solution.py:338
  32.5 0.2 collective-permute-start.7
  32.7 0.5 %collective-permute-start.6 = (f32[1,256]{1,0:T(1,128)S(1)}, f32[1,256]{1,0:T(1,128)S(1)}, u32[]{:S(2)}, u32[]{:S(2)}) collective-permute-start(f32[1,256]{1,0:T(1,128)S(1)} %get-tuple-element.25.own_ref), channel_id=1, source_target_pairs={{0,8},{8,0},{16,24},{24,16},{1,9},{9,1},{17,25},{25,17},{2,10},{10... | collective-permute-start | bytes 3080 | tf_op jit(solution)/shard_map/ppermute | solution.py:338
  33.2 8.0 %gradient.1 = (bf16[19008,256]{1,0:T(8,128)(2,1)}, f32[1,256]{1,0:T(1,128)}) custom-call(s32[9]{0:T(128)S(1)} %get-tuple-element.16.flag_ref, f32[1,256]{1,0:T(1,128)S(1)} %get-tuple-element.26.lse_ref, f32[1,256]{1,0:T(1,128)S(1)} %get-tuple-element.25.own_ref, s32[64,256]{1,0:T(8,128)S(1)} %get-tuple-element.18.local_ref, ...), custom_call_target="tpu_custom_call" | custom-call | tf_op jit(solution)/shard_map/gradient/pallas_call | solution.py:421
  41.2 0.0 collective-permute-done.8
  41.2 0.0 collective-permute-done.7
  41.2 0.0 collective-permute-done.6
  41.2 0.6 %add_reduce_fusion = f32[]{:T(128)} fusion(f32[1,256]{1,0:T(1,128)S(1)} %collective-permute-done.7, f32[1,256]{1,0:T(1,128)S(1)} %collective-permute-done.8, f32[1,256]{1,0:T(1,128)S(1)} %get-tuple-element.25.own_ref, f32[1,256]{1,0:T(1,128)S(1)} %collective-permute-done.6), kind=kLoop, calls=%fused_computation.12 | loop fusion | flops 1023 | bytes 4100 | tf_op jit(solution)/shard_map/reduce_sum | solution.py:439
  (4 shorter events, 0.0 us)
Async XLA Ops:
  0.6 12.1 %copy-start.1 = (s32[256,64]{0,1:T(8,128)S(1)}, s32[256,64]{0,1:T(8,128)}, u32[]{:S(2)}) copy-start(s32[256,64]{0,1:T(8,128)} %param.7) | copy-start | bytes 196612
  2.2 10.6 %copy-start = (f32[72,256]{1,0:T(8,128)S(1)}, f32[72,256]{1,0:T(8,128)}, u32[]{:S(2)}) copy-start(f32[72,256]{1,0:T(8,128)} %prepare.1.refs_0_) | copy-start | bytes 221188
  2.2 10.5 %collective-permute-start.2 = (f32[72,256]{1,0:T(8,128)}, f32[72,256]{1,0:T(8,128)S(1)}, u32[]{:S(2)}, u32[]{:S(2)}) collective-permute-start(f32[72,256]{1,0:T(8,128)} %prepare.1.refs_0_), channel_id=1, source_target_pairs={{0,24},{8,16},{16,8},{24,0},{1,25},{9,17},{17,9},{25,1},{2,26},{10... | collective-permute-start | bytes 221192 | tf_op jit(solution)/shard_map/ppermute | solution.py:338
  6.1 6.6 %collective-permute-start.1 = (f32[72,256]{1,0:T(8,128)}, f32[72,256]{1,0:T(8,128)S(1)}, u32[]{:S(2)}, u32[]{:S(2)}) collective-permute-start(f32[72,256]{1,0:T(8,128)} %prepare.1.refs_0_), channel_id=1, source_target_pairs={{0,16},{8,24},{16,0},{24,8},{1,17},{9,25},{17,1},{25,9},{2,18},{10... | collective-permute-start | bytes 221192 | tf_op jit(solution)/shard_map/ppermute | solution.py:338
  6.6 6.1 %collective-permute-start = (f32[72,256]{1,0:T(8,128)}, f32[72,256]{1,0:T(8,128)S(1)}, u32[]{:S(2)}, u32[]{:S(2)}) collective-permute-start(f32[72,256]{1,0:T(8,128)} %prepare.1.refs_0_), channel_id=1, source_target_pairs={{0,8},{8,0},{16,24},{24,16},{1,9},{9,1},{17,25},{25,17},{2,10},{10... | collective-permute-start | bytes 221192 | tf_op jit(solution)/shard_map/ppermute | solution.py:338
  19.9 1.2 %collective-permute-start.3 = (f32[8,256]{1,0:T(8,128)S(1)}, f32[8,256]{1,0:T(8,128)S(1)}, u32[]{:S(2)}, u32[]{:S(2)}) collective-permute-start(f32[8,256]{1,0:T(8,128)S(1)} %get-tuple-element.17), channel_id=1, source_target_pairs={{0,1},{1,0},{2,3},{3,2},{4,5},{5,4},{6,7},{7,6},{8,9},{9,8},{10,11... | collective-permute-start | bytes 24584 | tf_op jit(solution)/shard_map/ppermute | solution.py:415
  21.2 3.7 %collective-permute-start.4 = (f32[8,256]{1,0:T(8,128)S(1)}, f32[8,256]{1,0:T(8,128)S(1)}, u32[]{:S(2)}, u32[]{:S(2)}) collective-permute-start(f32[8,256]{1,0:T(8,128)S(1)} %maximum_maximum_fusion), channel_id=1, source_target_pairs={{0,2},{1,3},{2,0},{3,1},{4,6},{5,7},{6,4},{7,5},{8,10},{9,11},{10,... | collective-permute-start | bytes 24584 | tf_op jit(solution)/shard_map/ppermute | solution.py:415
  25.0 4.6 %collective-permute-start.5 = (f32[8,256]{1,0:T(8,128)S(1)}, f32[8,256]{1,0:T(8,128)S(1)}, u32[]{:S(2)}, u32[]{:S(2)}) collective-permute-start(f32[8,256]{1,0:T(8,128)S(1)} %maximum_maximum_fusion.1), channel_id=1, source_target_pairs={{0,4},{1,5},{2,6},{3,7},{4,0},{5,1},{6,2},{7,3},{8,12},{9,13},{10,... | collective-permute-start | bytes 24584 | tf_op jit(solution)/shard_map/ppermute | solution.py:415
  29.5 11.7 %collective-permute-start.8 = (f32[1,256]{1,0:T(1,128)S(1)}, f32[1,256]{1,0:T(1,128)S(1)}, u32[]{:S(2)}, u32[]{:S(2)}) collective-permute-start(f32[1,256]{1,0:T(1,128)S(1)} %get-tuple-element.25.own_ref), channel_id=1, source_target_pairs={{0,24},{8,16},{16,8},{24,0},{1,25},{9,17},{17,9},{25,1},{2,26},{10... | collective-permute-start | bytes 3080 | tf_op jit(solution)/shard_map/ppermute | solution.py:338
  32.5 8.7 %collective-permute-start.7 = (f32[1,256]{1,0:T(1,128)S(1)}, f32[1,256]{1,0:T(1,128)S(1)}, u32[]{:S(2)}, u32[]{:S(2)}) collective-permute-start(f32[1,256]{1,0:T(1,128)S(1)} %get-tuple-element.25.own_ref), channel_id=1, source_target_pairs={{0,16},{8,24},{16,0},{24,8},{1,17},{9,25},{17,1},{25,9},{2,18},{10... | collective-permute-start | bytes 3080 | tf_op jit(solution)/shard_map/ppermute | solution.py:338
  32.7 8.5 %collective-permute-start.6 = (f32[1,256]{1,0:T(1,128)S(1)}, f32[1,256]{1,0:T(1,128)S(1)}, u32[]{:S(2)}, u32[]{:S(2)}) collective-permute-start(f32[1,256]{1,0:T(1,128)S(1)} %get-tuple-element.25.own_ref), channel_id=1, source_target_pairs={{0,8},{8,0},{16,24},{24,16},{1,9},{9,1},{17,25},{25,17},{2,10},{10... | collective-permute-start | bytes 3080 | tf_op jit(solution)/shard_map/ppermute | solution.py:338

commit v3 on v2

--- a/solution.py
+++ b/solution.py
@@ -12,7 +12,7 @@
 LANE_ROWS = 16
 DEPTH = 3
 UNROLL = 4
-VMEM_BYTES = 32 * 1024 * 1024
+VMEM_BYTES = 13 * 1024 * 1024
 
 
 def largest_block(rows, limit):
@@ -26,6 +26,10 @@
 
 def any_spec():
     return pl.BlockSpec(memory_space=pltpu.HBM)
+
+
+def in_hbm(array):
+    return pltpu.with_memory_space_constraint(array, pltpu.HBM)
 
 
 def vmem_spec():
@@ -46,7 +50,7 @@
     out_ref[children:, :] = jnp.broadcast_to(owner_ref[...].astype(jnp.float32), (extra, rows))
 
 
-def stats_kernel(block, x_hbm, out_ref, x_ref, sems):
+def stats_kernel(block, x_hbm, out_ref, x_ref, power_ref, top_ref, sems):
     total, lanes = x_ref.shape
     blocks = total // block
     units = block // LANE_ROWS
@@ -58,17 +62,23 @@
     for index in range(blocks):
         copy(index).start()
 
+    def view(ref, index):
+        return ref.at[pl.ds(pl.multiple_of(index * block, LANE_ROWS), block), :]
+
     def block_top(index, best):
-        base = pl.multiple_of(index * block, LANE_ROWS)
+        x = view(x_ref, index)
         for i in range(units):
-            best = jnp.maximum(best, x_ref[pl.ds(base + i * LANE_ROWS, LANE_ROWS), :])
+            best = jnp.maximum(best, x[i * LANE_ROWS : (i + 1) * LANE_ROWS, :])
         return best
 
     def block_sum(index, wide, acc):
-        base = pl.multiple_of(index * block, LANE_ROWS)
+        x, powers = view(x_ref, index), view(power_ref, index)
+        top_ref[pl.ds(pl.multiple_of(index * LANE_ROWS, LANE_ROWS), LANE_ROWS), :] = wide
         for i in range(units):
-            values = x_ref[pl.ds(base + i * LANE_ROWS, LANE_ROWS), :].astype(jnp.float32)
-            acc = acc + jnp.exp2((values - wide) * LOG2E)
+            row = slice(i * LANE_ROWS, (i + 1) * LANE_ROWS)
+            power = jnp.exp2((x[row, :].astype(jnp.float32) - wide) * LOG2E)
+            powers[row, :] = power
+            acc = acc + power
         return acc
 
     def one(index, carry):
@@ -104,11 +114,9 @@
 
 def lists_kernel(leaf_blocks, bucket, group, *refs):
     routed = refs[:leaf_blocks]
-    ids_ref, stats_ref, x_ref = refs[leaf_blocks : leaf_blocks + 3]
-    local_ref, targets_ref, index_ref, share_ref, value_ref, flag_ref, out_ref = refs[
-        leaf_blocks + 3 : leaf_blocks + 10
-    ]
-    code_ref, rank_ref, slot_ref, at_ref, part_ref = refs[leaf_blocks + 10 :]
+    ids_ref, stats_ref, x_ref, _, *results = refs[leaf_blocks:]
+    local_ref, targets_ref, index_ref, share_ref, value_ref, flag_ref, out_ref = results[:7]
+    code_ref, rank_ref, slot_ref, at_ref, part_ref = results[7:]
     f32 = jnp.float32
     total, lanes = x_ref.shape
     children = ids_ref.shape[0]
@@ -169,14 +177,16 @@
         )
     targets_ref[...] = parts[:children] + parts[children : 2 * children] + parts[2 * children :]
 
-    for g in range(groups):
-        flag_ref[g] = 0
+    for b in range(buckets):
+        flag_ref[b] = 0
 
     @pl.when(deepest >= DEPTH)
     def _():
         for g in range(groups):
             over = (depth >= DEPTH) & (slot >= g * slots) & (slot < (g + 1) * slots)
-            flag_ref[g] = jnp.max(jnp.where(over, 1.0, 0.0)).astype(jnp.int32)
+            flag = jnp.max(jnp.where(over, 1.0, 0.0)).astype(jnp.int32)
+            for b in range(g * group, (g + 1) * group):
+                flag_ref[b] = flag
 
     steps = [(count + UNROLL - 1) // UNROLL for count in counts]
     for k in range(DEPTH):
@@ -235,8 +245,9 @@
         def fast():
             index = [index_ref[k, at_rows, :] for k in range(DEPTH)]
             found = [jnp.zeros((LANE_ROWS, lanes), jnp.bfloat16)] * DEPTH
+            x = x_ref.at[pl.ds(base, bucket), :]
             for i in range(units):
-                values = x_ref[pl.ds(base + i * LANE_ROWS, LANE_ROWS), :]
+                values = x[i * LANE_ROWS : (i + 1) * LANE_ROWS, :]
                 mark = jnp.bfloat16(i)
                 found = [jnp.where(index[k] == mark, values, found[k]) for k in range(DEPTH)]
             extra = jnp.zeros((LANE_ROWS, lanes), f32)
@@ -257,7 +268,7 @@
                 value_ref[k, at_rows, :] = zero.astype(jnp.bfloat16)
             return lax.fori_loop(0, units, add, zero)
 
-        return picked + lax.cond(flag_ref[b // group] == 0, fast, slow)
+        return picked + lax.cond(flag_ref[b] == 0, fast, slow)
 
     picked = lax.fori_loop(0, buckets, pick, jnp.zeros((LANE_ROWS, lanes), f32))
     out_ref[2:3, :] = jnp.sum(picked, axis=0, keepdims=True)
@@ -265,7 +276,6 @@
 
 def gradient_kernel(
     bucket,
-    group,
     flag_ref,
     lse_ref,
     own_ref,
@@ -274,27 +284,31 @@
     index_ref,
     share_ref,
     value_ref,
-    x_ref,
+    power_ref,
+    top_ref,
     out_hbm,
-    loss_ref,
+    loss_hbm,
     out_ref,
     sems,
+    loss_sem,
 ):
-    total, lanes = x_ref.shape
+    total, lanes = power_ref.shape
     buckets = total // bucket
 
     def back(index):
         window = pl.ds(index * bucket, bucket)
         return pltpu.make_async_copy(out_ref.at[window, :], out_hbm.at[window, :], sems.at[index])
 
-    loss_ref[...] = own_ref[...]
+    losses = pltpu.make_async_copy(own_ref, loss_hbm, loss_sem)
+    losses.start()
     lse = jnp.broadcast_to(lse_ref[0:1, :], (LANE_ROWS, lanes))
 
     def one(b, carry):
         base = pl.multiple_of(b * bucket, LANE_ROWS)
         at = pl.ds(pl.multiple_of(b * LANE_ROWS, LANE_ROWS), LANE_ROWS)
-
-        @pl.when(flag_ref[b // group] == 0)
+        scale = jnp.exp2((top_ref[at, :] - lse) * LOG2E)
+
+        @pl.when(flag_ref[b] == 0)
         def _():
             index = [index_ref[k, at, :] for k in range(DEPTH)]
             given = []
@@ -302,23 +316,23 @@
                 value = value_ref[k, at, :].astype(jnp.float32)
                 soft = jnp.exp2((value - lse) * LOG2E)
                 given.append((soft - share_ref[k, at, :]).astype(jnp.bfloat16))
+            powers = power_ref.at[pl.ds(base, bucket), :]
+            results = out_ref.at[pl.ds(base, bucket), :]
             for i in range(bucket // LANE_ROWS):
-                row = pl.ds(base + i * LANE_ROWS, LANE_ROWS)
-                values = x_ref[row, :].astype(jnp.float32)
-                result = jnp.exp2((values - lse) * LOG2E).astype(jnp.bfloat16)
+                row = slice(i * LANE_ROWS, (i + 1) * LANE_ROWS)
+                result = (powers[row, :] * scale).astype(jnp.bfloat16)
                 mark = jnp.bfloat16(i)
                 for k in range(DEPTH):
                     result = jnp.where(index[k] == mark, given[k], result)
-                out_ref[row, :] = result
-
-        @pl.when(flag_ref[b // group] != 0)
+                results[row, :] = result
+
+        @pl.when(flag_ref[b] != 0)
         def _():
             def fill(i, unused):
                 first = pl.multiple_of(base + i * LANE_ROWS, LANE_ROWS)
                 dense = dense_rows(local_ref, targets_ref, first, (LANE_ROWS, lanes))
                 row = pl.ds(first, LANE_ROWS)
-                values = x_ref[row, :].astype(jnp.float32)
-                out_ref[row, :] = (jnp.exp2((values - lse) * LOG2E) - dense).astype(jnp.bfloat16)
+                out_ref[row, :] = (power_ref[row, :] * scale - dense).astype(jnp.bfloat16)
                 return unused
 
             lax.fori_loop(0, bucket // LANE_ROWS, fill, 0)
@@ -329,6 +343,7 @@
     lax.fori_loop(0, buckets, one, 0)
     for index in range(buckets):
         back(index).wait()
+    losses.wait()
 
 
 def shifted(value, axis, size):
@@ -358,30 +373,33 @@
     leaf = pl.pallas_call(
         prepare_kernel,
         out_shape=jax.ShapeDtypeStruct((children + 8, lanes), f32),
+        compiler_params=params,
         name="prepare",
     )(
-        leaf_counts.T,
-        leaf_valid.reshape(1, lanes),
-        leaf_temp.reshape(1, lanes),
-        leaf_owner.reshape(1, lanes),
+        in_hbm(leaf_counts.T),
+        in_hbm(leaf_valid.reshape(1, lanes)),
+        in_hbm(leaf_temp.reshape(1, lanes)),
+        in_hbm(leaf_owner.reshape(1, lanes)),
     )
     routed = [leaf] + shifted(leaf, "dp", groups)
 
     bucket = largest_block(columns, 704)
     buckets = columns // bucket
     group = 3 if buckets % 3 == 0 else 1
-    stats, x = pl.pallas_call(
+    stats, x, power, tops = pl.pallas_call(
         functools.partial(stats_kernel, bucket),
         out_shape=(
             jax.ShapeDtypeStruct((8, lanes), f32),
             jax.ShapeDtypeStruct((columns, lanes), jnp.bfloat16),
+            jax.ShapeDtypeStruct((columns, lanes), f32),
+            jax.ShapeDtypeStruct((buckets * LANE_ROWS, lanes), f32),
         ),
         in_specs=[any_spec()],
-        out_specs=(vmem_spec(), vmem_spec()),
+        out_specs=(vmem_spec(),) * 4,
         scratch_shapes=[pltpu.SemaphoreType.DMA((buckets,))],
         compiler_params=params,
         name="stats",
-    )(pltpu.with_memory_space_constraint(logits.T, pltpu.HBM))
+    )(in_hbm(logits.T))
 
     listed = (DEPTH, buckets * LANE_ROWS, lanes)
     compact = DEPTH * children + 8
@@ -393,10 +411,10 @@
             jax.ShapeDtypeStruct(listed, jnp.bfloat16),
             jax.ShapeDtypeStruct(listed, f32),
             jax.ShapeDtypeStruct(listed, jnp.bfloat16),
-            jax.ShapeDtypeStruct((buckets // group,), jnp.int32),
+            jax.ShapeDtypeStruct((buckets,), jnp.int32),
             jax.ShapeDtypeStruct((8, lanes), f32),
         ),
-        in_specs=[vmem_spec()] * (groups + 3),
+        in_specs=[vmem_spec()] * (groups + 4),
         out_specs=(vmem_spec(),) * 5 + (smem_spec(), vmem_spec()),
         scratch_shapes=[
             pltpu.VMEM((children, lanes), jnp.int32),
@@ -407,7 +425,7 @@
         ],
         compiler_params=params,
         name="lists",
-    )(*routed, ids, stats, x)
+    )(*routed, ids, stats, x, power)
 
     hop = 1
     while hop < shards:
@@ -419,20 +437,21 @@
     others = shifted(own, "dp", groups)
 
     gradient, row_loss = pl.pallas_call(
-        functools.partial(gradient_kernel, bucket, group),
+        functools.partial(gradient_kernel, bucket),
         out_shape=(
             jax.ShapeDtypeStruct((columns, lanes), jnp.bfloat16),
             jax.ShapeDtypeStruct((1, lanes), f32),
         ),
-        in_specs=[smem_spec()] + [vmem_spec()] * 8,
-        out_specs=(any_spec(), vmem_spec()),
+        in_specs=[smem_spec()] + [vmem_spec()] * 9,
+        out_specs=(any_spec(), any_spec()),
         scratch_shapes=[
             pltpu.VMEM((columns, lanes), jnp.bfloat16),
             pltpu.SemaphoreType.DMA((buckets,)),
+            pltpu.SemaphoreType.DMA(()),
         ],
         compiler_params=params,
         name="gradient",
-    )(flags, lse, own, local, targets, index, share, value, x)
+    )(flags, lse, own, local, targets, index, share, value, power, tops)
     losses = [own] + others
     while len(losses) > 1:
         losses = [losses[i] + losses[i + 1] for i in range(0, len(losses), 2)]

time: 43.8 us -> 39.7 us (0.906)
  Pallas kernels: 22.6 us -> 18.6 us
    pallas_call x1, Pallas kernels: 8 us -> 5.24 us  [body(): pl.pallas_call(functools.partial(gradient_kernel, bucket), out_shape=(jax...]
    pallas_call x1, Pallas kernels: 7.07 us -> 6.43 us  [body(): pl.pallas_call(functools.partial(lists_kernel, groups, bucket, group), ou...]
    pallas_call x1, Pallas kernels: 1.57 us -> 0.93 us  [body(): pl.pallas_call(prepare_kernel, out_shape=jax.ShapeDtypeStruct((children +...]
  transfers between devices with their start and end apart: 9 -> 9, of which waited for: 3 -> 3; matrix products, arithmetic and copies ran while one was open for 0% -> 0% of each run, Pallas kernels for 32% -> 28%
where the time goes in v3:
time: 39.7 us; the launch traced here: 39.5 us
  Pallas kernels  18.6 us (47%)
  starting transfers between devices  12.6 us (32%)
  waiting for transfers between devices  4.91 us (12%)
  between operations  2.53 us (6%)
  other arithmetic  0.79 us (2%)
    ppermute x6, starting transfers between devices, shifted(): result.append(lax.ppermute(value, axis, pairs))  8.13 us
    pallas_call x1, Pallas kernels, body(): pl.pallas_call(functools.partial(lists_kernel, groups, bucket, group), ou...  6.43 us
    pallas_call x1, Pallas kernels, body(): pl.pallas_call(functools.partial(stats_kernel, bucket), out_shape=(jax.Sh...  5.95 us
    pallas_call x1, Pallas kernels, body(): pl.pallas_call(functools.partial(gradient_kernel, bucket), out_shape=(jax...  5.24 us
    ppermute x3, waiting for transfers between devices, body(): sums = merge(sums, lax.ppermute(sums, 'tensor', pairs))  4.89 us
    ppermute x3, starting transfers between devices, body(): sums = merge(sums, lax.ppermute(sums, 'tensor', pairs))  4.48 us
    pallas_call x1, Pallas kernels, body(): pl.pallas_call(prepare_kernel, out_shape=jax.ShapeDtypeStruct((children +...  0.93 us
  transfers between devices with their start and end apart: 9, of which 3 were waited for; matrix products, arithmetic and copies ran while one was open for 0% of the time, Pallas kernels for 28%

profile of v3, /device:TPU:0, one launch (start us, length us, event | category | flops | bytes accessed | tf_op | source)
XLA Modules:
  0.0 39.5 jit_solution(11281212007297880277)
XLA Ops:
  0.6 0.0 copy-start
  0.6 0.9 %prepare.1.refs_0_ = f32[72,256]{1,0:T(8,128)S(1)} custom-call(s32[64,256]{1,0:T(8,128)} %bitcast.10, s32[1,256]{1,0:T(1,128)} %bitcast.11, f32[1,256]{1,0:T(1,128)} %bitcast.12, s32[1,256]{1,0:T(1,128)} %bitcast.13), custom_call_target="tpu_custom_call" | custom-call | tf_op jit(solution)/shard_map/prepare/pallas_call | solution.py:373
  1.6 3.0 %collective-permute-start = (f32[72,256]{1,0:T(8,128)S(1)}, f32[72,256]{1,0:T(8,128)S(1)}, u32[]{:S(2)}, u32[]{:S(2)}) collective-permute-start(f32[72,256]{1,0:T(8,128)S(1)} %prepare.1.refs_0_), channel_id=1, source_target_pairs={{0,8},{8,0},{16,24},{24,16},{1,9},{9,1},{17,25},{25,17},{2,10},{10... | collective-permute-start | bytes 221192 | tf_op jit(solution)/shard_map/ppermute | solution.py:353
  4.6 1.5 %collective-permute-start.1 = (f32[72,256]{1,0:T(8,128)S(1)}, f32[72,256]{1,0:T(8,128)S(1)}, u32[]{:S(2)}, u32[]{:S(2)}) collective-permute-start(f32[72,256]{1,0:T(8,128)S(1)} %prepare.1.refs_0_), channel_id=1, source_target_pairs={{0,16},{8,24},{16,0},{24,8},{1,17},{9,25},{17,1},{25,9},{2,18},{10... | collective-permute-start | bytes 221192 | tf_op jit(solution)/shard_map/ppermute | solution.py:353
  6.1 0.0 collective-permute-start.2
  6.2 6.0 %stats.1 = (f32[8,256]{1,0:T(8,128)S(1)}, bf16[19008,256]{1,0:T(8,128)(2,1)S(1)}, f32[19008,256]{1,0:T(8,128)S(1)}, f32[432,256]{1,0:T(8,128)S(1)}) custom-call(bf16[19008,256]{1,0:T(8,128)(2,1)} %bitcast.9), custom_call_target="tpu_custom_call" | custom-call | tf_op jit(solution)/shard_map/stats/pallas_call | solution.py:389
  12.1 0.0 collective-permute-done.refs_1_
  12.1 0.0 collective-permute-done.1.refs_2_
  12.1 0.0 collective-permute-done.2.refs_3_
  12.1 0.0 copy-done
  12.2 6.4 %lists.1 = (s32[64,256]{1,0:T(8,128)S(1)}, f32[64,256]{1,0:T(8,128)S(1)}, bf16[3,432,256]{2,1,0:T(8,128)(2,1)S(1)}, f32[3,432,256]{2,1,0:T(8,128)S(1)}, bf16[3,4...) custom-call(f32[72,256]{1,0:T(8,128)S(1)} %prepare.1.refs_0_, ...), custom_call_target="tpu_custom_call" | custom-call | tf_op jit(solution)/shard_map/lists/pallas_call | solution.py:406
  18.6 0.1 collective-permute-start.3
  18.7 0.1 pad.7.clone
  18.8 1.1 %collective-permute-done.3 = f32[8,256]{1,0:T(8,128)S(1)} collective-permute-done((f32[8,256]{1,0:T(8,128)S(1)}, f32[8,256]{1,0:T(8,128)S(1)}, u32[]{:S(2)}, u32[]{:S(2)}) %collective-permute-start.3) | collective-permute-done | bytes 8224 | tf_op jit(solution)/shard_map/ppermute | solution.py:433
  19.8 0.1 maximum_maximum_fusion
  19.9 1.7 %collective-permute-start.4 = (f32[8,256]{1,0:T(8,128)S(1)}, f32[8,256]{1,0:T(8,128)S(1)}, u32[]{:S(2)}, u32[]{:S(2)}) collective-permute-start(f32[8,256]{1,0:T(8,128)S(1)} %maximum_maximum_fusion), channel_id=1, source_target_pairs={{0,2},{1,3},{2,0},{3,1},{4,6},{5,7},{6,4},{7,5},{8,10},{9,11},{10,... | collective-permute-start | bytes 24584 | tf_op jit(solution)/shard_map/ppermute | solution.py:433
  21.6 2.0 %collective-permute-done.4 = f32[8,256]{1,0:T(8,128)S(1)} collective-permute-done((f32[8,256]{1,0:T(8,128)S(1)}, f32[8,256]{1,0:T(8,128)S(1)}, u32[]{:S(2)}, u32[]{:S(2)}) %collective-permute-start.4) | collective-permute-done | bytes 8224 | tf_op jit(solution)/shard_map/ppermute | solution.py:433
  23.6 0.1 maximum_maximum_fusion.1
  23.7 2.7 %collective-permute-start.5 = (f32[8,256]{1,0:T(8,128)S(1)}, f32[8,256]{1,0:T(8,128)S(1)}, u32[]{:S(2)}, u32[]{:S(2)}) collective-permute-start(f32[8,256]{1,0:T(8,128)S(1)} %maximum_maximum_fusion.1), channel_id=1, source_target_pairs={{0,4},{1,5},{2,6},{3,7},{4,0},{5,1},{6,2},{7,3},{8,12},{9,13},{10,... | collective-permute-start | bytes 24584 | tf_op jit(solution)/shard_map/ppermute | solution.py:433
  26.4 1.9 %collective-permute-done.5 = f32[8,256]{1,0:T(8,128)S(1)} collective-permute-done((f32[8,256]{1,0:T(8,128)S(1)}, f32[8,256]{1,0:T(8,128)S(1)}, u32[]{:S(2)}, u32[]{:S(2)}) %collective-permute-start.5) | collective-permute-done | bytes 8224 | tf_op jit(solution)/shard_map/ppermute | solution.py:433
  28.2 1.7 %collective-permute-start.6 = (f32[1,256]{1,0:T(1,128)S(1)}, f32[1,256]{1,0:T(1,128)S(1)}, u32[]{:S(2)}, u32[]{:S(2)}) collective-permute-start(f32[1,256]{1,0:T(1,128)S(1)} %get-tuple-element.29.own_ref), channel_id=1, source_target_pairs={{0,8},{8,0},{16,24},{24,16},{1,9},{9,1},{17,25},{25,17},{2,10},{10... | collective-permute-start | bytes 3080 | tf_op jit(solution)/shard_map/ppermute | solution.py:353
  29.9 1.8 %collective-permute-start.7 = (f32[1,256]{1,0:T(1,128)S(1)}, f32[1,256]{1,0:T(1,128)S(1)}, u32[]{:S(2)}, u32[]{:S(2)}) collective-permute-start(f32[1,256]{1,0:T(1,128)S(1)} %get-tuple-element.29.own_ref), channel_id=1, source_target_pairs={{0,16},{8,24},{16,0},{24,8},{1,17},{9,25},{17,1},{25,9},{2,18},{10... | collective-permute-start | bytes 3080 | tf_op jit(solution)/shard_map/ppermute | solution.py:353
  31.7 0.1 collective-permute-start.8
  31.8 5.2 %gradient.1 = (bf16[19008,256]{1,0:T(8,128)(2,1)}, f32[1,256]{1,0:T(1,128)}) custom-call(s32[27]{0:T(128)S(1)} %get-tuple-element.19.flag_ref, f32[1,256]{1,0:T(1,128)S(1)} %get-tuple-element.30.lse_ref, f32[1,256]{1,0:T(1,128)S(1)} %get-tuple-element.29.own_ref, s32[64,256]{1,0:T(8,128)S(1)} %get-tuple-element.21.local_ref, ...), custom_call_target="tpu_custom_call" | custom-call | tf_op jit(solution)/shard_map/gradient/pallas_call | solution.py:439
  37.1 0.0 collective-permute-done.6
  37.1 0.0 collective-permute-done.7
  37.1 0.0 collective-permute-done.8
  37.1 0.6 %add_reduce_fusion = f32[]{:T(128)} fusion(f32[1,256]{1,0:T(1,128)S(1)} %collective-permute-done.7, f32[1,256]{1,0:T(1,128)S(1)} %collective-permute-done.8, f32[1,256]{1,0:T(1,128)S(1)} %get-tuple-element.29.own_ref, f32[1,256]{1,0:T(1,128)S(1)} %collective-permute-done.6), kind=kLoop, calls=%fused_computation.12 | loop fusion | flops 1023 | bytes 4100 | tf_op jit(solution)/shard_map/reduce_sum | solution.py:458
  (4 shorter events, 0.0 us)
Async XLA Ops:
  0.6 11.5 %copy-start = (s32[256,64]{0,1:T(8,128)S(1)}, s32[256,64]{0,1:T(8,128)}, u32[]{:S(2)}) copy-start(s32[256,64]{0,1:T(8,128)} %param.7) | copy-start | bytes 196612
  1.6 10.5 %collective-permute-start = (f32[72,256]{1,0:T(8,128)S(1)}, f32[72,256]{1,0:T(8,128)S(1)}, u32[]{:S(2)}, u32[]{:S(2)}) collective-permute-start(f32[72,256]{1,0:T(8,128)S(1)} %prepare.1.refs_0_), channel_id=1, source_target_pairs={{0,8},{8,0},{16,24},{24,16},{1,9},{9,1},{17,25},{25,17},{2,10},{10... | collective-permute-start | bytes 221192 | tf_op jit(solution)/shard_map/ppermute | solution.py:353
  4.6 7.5 %collective-permute-start.1 = (f32[72,256]{1,0:T(8,128)S(1)}, f32[72,256]{1,0:T(8,128)S(1)}, u32[]{:S(2)}, u32[]{:S(2)}) collective-permute-start(f32[72,256]{1,0:T(8,128)S(1)} %prepare.1.refs_0_), channel_id=1, source_target_pairs={{0,16},{8,24},{16,0},{24,8},{1,17},{9,25},{17,1},{25,9},{2,18},{10... | collective-permute-start | bytes 221192 | tf_op jit(solution)/shard_map/ppermute | solution.py:353
  6.1 6.0 %collective-permute-start.2 = (f32[72,256]{1,0:T(8,128)S(1)}, f32[72,256]{1,0:T(8,128)S(1)}, u32[]{:S(2)}, u32[]{:S(2)}) collective-permute-start(f32[72,256]{1,0:T(8,128)S(1)} %prepare.1.refs_0_), channel_id=1, source_target_pairs={{0,24},{8,16},{16,8},{24,0},{1,25},{9,17},{17,9},{25,1},{2,26},{10... | collective-permute-start | bytes 221192 | tf_op jit(solution)/shard_map/ppermute | solution.py:353
  18.6 1.2 %collective-permute-start.3 = (f32[8,256]{1,0:T(8,128)S(1)}, f32[8,256]{1,0:T(8,128)S(1)}, u32[]{:S(2)}, u32[]{:S(2)}) collective-permute-start(f32[8,256]{1,0:T(8,128)S(1)} %get-tuple-element.20), channel_id=1, source_target_pairs={{0,1},{1,0},{2,3},{3,2},{4,5},{5,4},{6,7},{7,6},{8,9},{9,8},{10,11... | collective-permute-start | bytes 24584 | tf_op jit(solution)/shard_map/ppermute | solution.py:433
  19.9 3.7 %collective-permute-start.4 = (f32[8,256]{1,0:T(8,128)S(1)}, f32[8,256]{1,0:T(8,128)S(1)}, u32[]{:S(2)}, u32[]{:S(2)}) collective-permute-start(f32[8,256]{1,0:T(8,128)S(1)} %maximum_maximum_fusion), channel_id=1, source_target_pairs={{0,2},{1,3},{2,0},{3,1},{4,6},{5,7},{6,4},{7,5},{8,10},{9,11},{10,... | collective-permute-start | bytes 24584 | tf_op jit(solution)/shard_map/ppermute | solution.py:433
  23.7 4.6 %collective-permute-start.5 = (f32[8,256]{1,0:T(8,128)S(1)}, f32[8,256]{1,0:T(8,128)S(1)}, u32[]{:S(2)}, u32[]{:S(2)}) collective-permute-start(f32[8,256]{1,0:T(8,128)S(1)} %maximum_maximum_fusion.1), channel_id=1, source_target_pairs={{0,4},{1,5},{2,6},{3,7},{4,0},{5,1},{6,2},{7,3},{8,12},{9,13},{10,... | collective-permute-start | bytes 24584 | tf_op jit(solution)/shard_map/ppermute | solution.py:433
  28.2 8.8 %collective-permute-start.6 = (f32[1,256]{1,0:T(1,128)S(1)}, f32[1,256]{1,0:T(1,128)S(1)}, u32[]{:S(2)}, u32[]{:S(2)}) collective-permute-start(f32[1,256]{1,0:T(1,128)S(1)} %get-tuple-element.29.own_ref), channel_id=1, source_target_pairs={{0,8},{8,0},{16,24},{24,16},{1,9},{9,1},{17,25},{25,17},{2,10},{10... | collective-permute-start | bytes 3080 | tf_op jit(solution)/shard_map/ppermute | solution.py:353
  29.9 7.2 %collective-permute-start.7 = (f32[1,256]{1,0:T(1,128)S(1)}, f32[1,256]{1,0:T(1,128)S(1)}, u32[]{:S(2)}, u32[]{:S(2)}) collective-permute-start(f32[1,256]{1,0:T(1,128)S(1)} %get-tuple-element.29.own_ref), channel_id=1, source_target_pairs={{0,16},{8,24},{16,0},{24,8},{1,17},{9,25},{17,1},{25,9},{2,18},{10... | collective-permute-start | bytes 3080 | tf_op jit(solution)/shard_map/ppermute | solution.py:353
  31.7 5.3 %collective-permute-start.8 = (f32[1,256]{1,0:T(1,128)S(1)}, f32[1,256]{1,0:T(1,128)S(1)}, u32[]{:S(2)}, u32[]{:S(2)}) collective-permute-start(f32[1,256]{1,0:T(1,128)S(1)} %get-tuple-element.29.own_ref), channel_id=1, source_target_pairs={{0,24},{8,16},{16,8},{24,0},{1,25},{9,17},{17,9},{25,1},{2,26},{10... | collective-permute-start | bytes 3080 | tf_op jit(solution)/shard_map/ppermute | solution.py:353

commit v4 on v3

--- a/solution.py
+++ b/solution.py
@@ -12,6 +12,8 @@
 LANE_ROWS = 16
 DEPTH = 3
 UNROLL = 4
+CHAINS = 4
+USUAL = 2
 VMEM_BYTES = 13 * 1024 * 1024
 
 
@@ -65,36 +67,35 @@
     def view(ref, index):
         return ref.at[pl.ds(pl.multiple_of(index * block, LANE_ROWS), block), :]
 
-    def block_top(index, best):
-        x = view(x_ref, index)
-        for i in range(units):
-            best = jnp.maximum(best, x[i * LANE_ROWS : (i + 1) * LANE_ROWS, :])
-        return best
-
-    def block_sum(index, wide, acc):
+    def block_pass(index, wide, acc, following, best):
+        top_ref[pl.ds(pl.multiple_of(index * LANE_ROWS, LANE_ROWS), LANE_ROWS), :] = wide
         x, powers = view(x_ref, index), view(power_ref, index)
-        top_ref[pl.ds(pl.multiple_of(index * LANE_ROWS, LANE_ROWS), LANE_ROWS), :] = wide
+        following = None if following is None else view(x_ref, following)
+        tops = [best] * CHAINS
         for i in range(units):
             row = slice(i * LANE_ROWS, (i + 1) * LANE_ROWS)
             power = jnp.exp2((x[row, :].astype(jnp.float32) - wide) * LOG2E)
             powers[row, :] = power
             acc = acc + power
-        return acc
+            if following is not None:
+                tops[i % CHAINS] = jnp.maximum(tops[i % CHAINS], following[row, :])
+        return acc, functools.reduce(jnp.maximum, tops)
 
     def one(index, carry):
         top, acc = carry
         copy(index + 1).wait()
-        new_top = block_top(index + 1, top)
         wide = top.astype(jnp.float32)
-        acc = block_sum(index, wide, acc)
+        acc, new_top = block_pass(index, wide, acc, index + 1, top)
         acc = acc * jnp.exp2((wide - new_top.astype(jnp.float32)) * LOG2E)
         return new_top, acc
 
     copy(0).wait()
-    top = block_top(0, jnp.full((LANE_ROWS, lanes), -3.0e38, jnp.bfloat16))
+    first = view(x_ref, 0)
+    tops = [first[i * LANE_ROWS : (i + 1) * LANE_ROWS, :] for i in range(units)]
+    top = functools.reduce(jnp.maximum, tops)
     top, acc = lax.fori_loop(0, blocks - 1, one, (top, jnp.zeros((LANE_ROWS, lanes), jnp.float32)))
     wide = top.astype(jnp.float32)
-    acc = block_sum(blocks - 1, wide, acc)
+    acc, _ = block_pass(blocks - 1, wide, acc, None, top)
     row_top = jnp.max(wide, axis=0, keepdims=True)
     row_sum = jnp.sum(acc * jnp.exp2((wide - row_top) * LOG2E), axis=0, keepdims=True)
     out_ref[0:1, :] = row_top
@@ -177,8 +178,12 @@
         )
     targets_ref[...] = parts[:children] + parts[children : 2 * children] + parts[2 * children :]
 
+    third = jnp.where(depth >= USUAL, at_bucket.astype(f32), -1.0)
+    last = jnp.max(third).astype(jnp.int32)
+    third = jnp.where(depth >= USUAL, at_bucket.astype(f32), 1.0 * buckets)
+    first = jnp.min(third).astype(jnp.int32)
     for b in range(buckets):
-        flag_ref[b] = 0
+        flag_ref[b] = jnp.where((first <= b) & (last >= b), 1, 0).astype(jnp.int32)
 
     @pl.when(deepest >= DEPTH)
     def _():
@@ -186,7 +191,7 @@
             over = (depth >= DEPTH) & (slot >= g * slots) & (slot < (g + 1) * slots)
             flag = jnp.max(jnp.where(over, 1.0, 0.0)).astype(jnp.int32)
             for b in range(g * group, (g + 1) * group):
-                flag_ref[b] = flag
+                flag_ref[b] = jnp.where(flag > 0, 2, flag_ref[b])
 
     steps = [(count + UNROLL - 1) // UNROLL for count in counts]
     for k in range(DEPTH):
@@ -205,10 +210,12 @@
 
         lax.fori_loop(0, steps[k], compact, 0)
 
-    def fill(g, unused):
+    def fill(g, unused, levels):
         slot_row = lax.broadcasted_iota(jnp.int32, (slots, lanes), 0) + g * slots
-        index, share = [], []
-        for k in range(DEPTH):
+        rows = pl.ds(pl.multiple_of(g * slots, LANE_ROWS), slots)
+        index = [index_ref[k, rows, :].astype(f32) for k in range(levels[0])]
+        share = [share_ref[k, rows, :] for k in range(levels[0])]
+        for k in levels:
 
             def add(step, carry, k=k):
                 found, amount = carry
@@ -229,29 +236,34 @@
                 amount = jnp.where(same, 0.0, amount)
             index.append(found)
             share.append(amount)
-        rows = pl.ds(pl.multiple_of(g * slots, LANE_ROWS), slots)
-        for k in range(DEPTH):
-            index_ref[k, rows, :] = index[k].astype(jnp.bfloat16)
+        for k in range(levels[-1] + 1):
+            if k in levels:
+                index_ref[k, rows, :] = index[k].astype(jnp.bfloat16)
             share_ref[k, rows, :] = share[k]
         return unused
 
-    lax.fori_loop(0, groups, fill, 0)
+    lax.fori_loop(0, groups, functools.partial(fill, levels=tuple(range(USUAL))), 0)
+
+    @pl.when(deepest >= USUAL)
+    def _():
+        lax.fori_loop(0, groups, functools.partial(fill, levels=tuple(range(USUAL, DEPTH))), 0)
+
     out_ref[...] = stats_ref[...]
 
     def pick(b, picked):
         base = pl.multiple_of(b * bucket, LANE_ROWS)
         at_rows = pl.ds(pl.multiple_of(b * LANE_ROWS, LANE_ROWS), LANE_ROWS)
 
-        def fast():
-            index = [index_ref[k, at_rows, :] for k in range(DEPTH)]
-            found = [jnp.zeros((LANE_ROWS, lanes), jnp.bfloat16)] * DEPTH
+        def fast(entries):
+            index = [index_ref[k, at_rows, :] for k in range(entries)]
+            found = [jnp.zeros((LANE_ROWS, lanes), jnp.bfloat16)] * entries
             x = x_ref.at[pl.ds(base, bucket), :]
             for i in range(units):
                 values = x[i * LANE_ROWS : (i + 1) * LANE_ROWS, :]
                 mark = jnp.bfloat16(i)
-                found = [jnp.where(index[k] == mark, values, found[k]) for k in range(DEPTH)]
+                found = [jnp.where(index[k] == mark, values, found[k]) for k in range(entries)]
             extra = jnp.zeros((LANE_ROWS, lanes), f32)
-            for k in range(DEPTH):
+            for k in range(entries):
                 value_ref[k, at_rows, :] = found[k]
                 extra = extra + share_ref[k, at_rows, :] * found[k].astype(f32)
             return extra
@@ -268,7 +280,10 @@
                 value_ref[k, at_rows, :] = zero.astype(jnp.bfloat16)
             return lax.fori_loop(0, units, add, zero)
 
-        return picked + lax.cond(flag_ref[b] == 0, fast, slow)
+        usual = functools.partial(fast, USUAL)
+        deeper = functools.partial(fast, DEPTH)
+        rare = lambda: lax.cond(flag_ref[b] == 1, deeper, slow)
+        return picked + lax.cond(flag_ref[b] == 0, usual, rare)
 
     picked = lax.fori_loop(0, buckets, pick, jnp.zeros((LANE_ROWS, lanes), f32))
     out_ref[2:3, :] = jnp.sum(picked, axis=0, keepdims=True)
@@ -308,11 +323,10 @@
         at = pl.ds(pl.multiple_of(b * LANE_ROWS, LANE_ROWS), LANE_ROWS)
         scale = jnp.exp2((top_ref[at, :] - lse) * LOG2E)
 
-        @pl.when(flag_ref[b] == 0)
-        def _():
-            index = [index_ref[k, at, :] for k in range(DEPTH)]
+        def listed(entries):
+            index = [index_ref[k, at, :] for k in range(entries)]
             given = []
-            for k in range(DEPTH):
+            for k in range(entries):
                 value = value_ref[k, at, :].astype(jnp.float32)
                 soft = jnp.exp2((value - lse) * LOG2E)
                 given.append((soft - share_ref[k, at, :]).astype(jnp.bfloat16))
@@ -322,11 +336,14 @@
                 row = slice(i * LANE_ROWS, (i + 1) * LANE_ROWS)
                 result = (powers[row, :] * scale).astype(jnp.bfloat16)
                 mark = jnp.bfloat16(i)
-                for k in range(DEPTH):
+                for k in range(entries):
                     result = jnp.where(index[k] == mark, given[k], result)
                 results[row, :] = result
 
-        @pl.when(flag_ref[b] != 0)
+        pl.when(flag_ref[b] == 0)(functools.partial(listed, USUAL))
+        pl.when(flag_ref[b] == 1)(functools.partial(listed, DEPTH))
+
+        @pl.when(flag_ref[b] == 2)
         def _():
             def fill(i, unused):
                 first = pl.multiple_of(base + i * LANE_ROWS, LANE_ROWS)

time: 39.7 us -> 37.9 us (0.955)
  Pallas kernels: 18.6 us -> 16.2 us
  starting transfers between devices: 12.6 us -> 13.8 us
  waiting for transfers between devices: 4.91 us -> 4.35 us
    pallas_call x1, Pallas kernels: 6.43 us -> 5.21 us  [body(): pl.pallas_call(functools.partial(lists_kernel, groups, bucket, group), ou...]
    ppermute x3, starting transfers between devices: 4.48 us -> 5.46 us  [body(): sums = merge(sums, lax.ppermute(sums, 'tensor', pairs))]
    pallas_call x1, Pallas kernels: 5.95 us -> 5.29 us  [body(): pl.pallas_call(functools.partial(stats_kernel, bucket), out_shape=(jax.Sh...]
    ppermute x3, waiting for transfers between devices: 4.89 us -> 4.33 us  [body(): sums = merge(sums, lax.ppermute(sums, 'tensor', pairs))]
    pallas_call x1, Pallas kernels: 5.24 us -> 4.76 us  [body(): pl.pallas_call(functools.partial(gradient_kernel, bucket), out_shape=(jax...]
  transfers between devices with their start and end apart: 9 -> 9, of which waited for: 3 -> 3; matrix products, arithmetic and copies ran while one was open for 0% -> 0% of each run, Pallas kernels for 28% -> 27%
where the time goes in v4:
time: 37.9 us; the launch traced here: 37.8 us
  Pallas kernels  16.2 us (43%)
  starting transfers between devices  13.8 us (36%)
  waiting for transfers between devices  4.35 us (11%)
  between operations  2.53 us (7%)
  other arithmetic  0.79 us (2%)
    ppermute x6, starting transfers between devices, shifted(): result.append(lax.ppermute(value, axis, pairs))  8.39 us
    ppermute x3, starting transfers between devices, body(): sums = merge(sums, lax.ppermute(sums, 'tensor', pairs))  5.46 us
    pallas_call x1, Pallas kernels, body(): pl.pallas_call(functools.partial(stats_kernel, bucket), out_shape=(jax.Sh...  5.29 us
    pallas_call x1, Pallas kernels, body(): pl.pallas_call(functools.partial(lists_kernel, groups, bucket, group), ou...  5.21 us
    pallas_call x1, Pallas kernels, body(): pl.pallas_call(functools.partial(gradient_kernel, bucket), out_shape=(jax...  4.76 us
    ppermute x3, waiting for transfers between devices, body(): sums = merge(sums, lax.ppermute(sums, 'tensor', pairs))  4.33 us
    pallas_call x1, Pallas kernels, body(): pl.pallas_call(prepare_kernel, out_shape=jax.ShapeDtypeStruct((children +...  0.93 us
  transfers between devices with their start and end apart: 9, of which 3 were waited for; matrix products, arithmetic and copies ran while one was open for 0% of the time, Pallas kernels for 27%

profile of v4, /device:TPU:0, one launch (start us, length us, event | category | flops | bytes accessed | tf_op | source)
XLA Modules:
  0.0 37.8 jit_solution(2303378877618612177)
XLA Ops:
  0.6 0.0 copy-start
  0.6 0.9 %prepare.1.refs_0_ = f32[72,256]{1,0:T(8,128)S(1)} custom-call(s32[64,256]{1,0:T(8,128)} %bitcast.10, s32[1,256]{1,0:T(1,128)} %bitcast.11, f32[1,256]{1,0:T(1,128)} %bitcast.12, s32[1,256]{1,0:T(1,128)} %bitcast.13), custom_call_target="tpu_custom_call" | custom-call | tf_op jit(solution)/shard_map/prepare/pallas_call | solution.py:390
  1.6 3.0 %collective-permute-start = (f32[72,256]{1,0:T(8,128)S(1)}, f32[72,256]{1,0:T(8,128)S(1)}, u32[]{:S(2)}, u32[]{:S(2)}) collective-permute-start(f32[72,256]{1,0:T(8,128)S(1)} %prepare.1.refs_0_), channel_id=1, source_target_pairs={{0,8},{8,0},{16,24},{24,16},{1,9},{9,1},{17,25},{25,17},{2,10},{10... | collective-permute-start | bytes 221192 | tf_op jit(solution)/shard_map/ppermute | solution.py:370
  4.6 1.5 %collective-permute-start.1 = (f32[72,256]{1,0:T(8,128)S(1)}, f32[72,256]{1,0:T(8,128)S(1)}, u32[]{:S(2)}, u32[]{:S(2)}) collective-permute-start(f32[72,256]{1,0:T(8,128)S(1)} %prepare.1.refs_0_), channel_id=1, source_target_pairs={{0,16},{8,24},{16,0},{24,8},{1,17},{9,25},{17,1},{25,9},{2,18},{10... | collective-permute-start | bytes 221192 | tf_op jit(solution)/shard_map/ppermute | solution.py:370
  6.1 0.0 collective-permute-start.2
  6.2 5.3 %stats.1 = (f32[8,256]{1,0:T(8,128)S(1)}, bf16[19008,256]{1,0:T(8,128)(2,1)S(1)}, f32[19008,256]{1,0:T(8,128)S(1)}, f32[432,256]{1,0:T(8,128)S(1)}) custom-call(bf16[19008,256]{1,0:T(8,128)(2,1)} %bitcast.9), custom_call_target="tpu_custom_call" | custom-call | tf_op jit(solution)/shard_map/stats/pallas_call | solution.py:406
  11.5 0.0 collective-permute-done.refs_1_
  11.5 0.0 collective-permute-done.1.refs_2_
  11.5 0.0 collective-permute-done.2.refs_3_
  11.5 0.0 copy-done
  11.5 5.2 %lists.1 = (s32[64,256]{1,0:T(8,128)S(1)}, f32[64,256]{1,0:T(8,128)S(1)}, bf16[3,432,256]{2,1,0:T(8,128)(2,1)S(1)}, f32[3,432,256]{2,1,0:T(8,128)S(1)}, bf16[3,4...) custom-call(f32[72,256]{1,0:T(8,128)S(1)} %prepare.1.refs_0_, ...), custom_call_target="tpu_custom_call" | custom-call | tf_op jit(solution)/shard_map/lists/pallas_call | solution.py:423
  16.7 0.1 collective-permute-start.3
  16.8 0.1 pad.7.clone
  16.9 1.1 %collective-permute-done.3 = f32[8,256]{1,0:T(8,128)S(1)} collective-permute-done((f32[8,256]{1,0:T(8,128)S(1)}, f32[8,256]{1,0:T(8,128)S(1)}, u32[]{:S(2)}, u32[]{:S(2)}) %collective-permute-start.3) | collective-permute-done | bytes 8224 | tf_op jit(solution)/shard_map/ppermute | solution.py:450
  18.0 0.1 maximum_maximum_fusion
  18.0 2.0 %collective-permute-start.4 = (f32[8,256]{1,0:T(8,128)S(1)}, f32[8,256]{1,0:T(8,128)S(1)}, u32[]{:S(2)}, u32[]{:S(2)}) collective-permute-start(f32[8,256]{1,0:T(8,128)S(1)} %maximum_maximum_fusion), channel_id=1, source_target_pairs={{0,2},{1,3},{2,0},{3,1},{4,6},{5,7},{6,4},{7,5},{8,10},{9,11},{10,... | collective-permute-start | bytes 24584 | tf_op jit(solution)/shard_map/ppermute | solution.py:450
  20.1 1.6 %collective-permute-done.4 = f32[8,256]{1,0:T(8,128)S(1)} collective-permute-done((f32[8,256]{1,0:T(8,128)S(1)}, f32[8,256]{1,0:T(8,128)S(1)}, u32[]{:S(2)}, u32[]{:S(2)}) %collective-permute-start.4) | collective-permute-done | bytes 8224 | tf_op jit(solution)/shard_map/ppermute | solution.py:450
  21.7 0.1 maximum_maximum_fusion.1
  21.8 3.3 %collective-permute-start.5 = (f32[8,256]{1,0:T(8,128)S(1)}, f32[8,256]{1,0:T(8,128)S(1)}, u32[]{:S(2)}, u32[]{:S(2)}) collective-permute-start(f32[8,256]{1,0:T(8,128)S(1)} %maximum_maximum_fusion.1), channel_id=1, source_target_pairs={{0,4},{1,5},{2,6},{3,7},{4,0},{5,1},{6,2},{7,3},{8,12},{9,13},{10,... | collective-permute-start | bytes 24584 | tf_op jit(solution)/shard_map/ppermute | solution.py:450
  25.1 1.6 %collective-permute-done.5 = f32[8,256]{1,0:T(8,128)S(1)} collective-permute-done((f32[8,256]{1,0:T(8,128)S(1)}, f32[8,256]{1,0:T(8,128)S(1)}, u32[]{:S(2)}, u32[]{:S(2)}) %collective-permute-start.5) | collective-permute-done | bytes 8224 | tf_op jit(solution)/shard_map/ppermute | solution.py:450
  26.8 2.3 %collective-permute-start.6 = (f32[1,256]{1,0:T(1,128)S(1)}, f32[1,256]{1,0:T(1,128)S(1)}, u32[]{:S(2)}, u32[]{:S(2)}) collective-permute-start(f32[1,256]{1,0:T(1,128)S(1)} %get-tuple-element.29.own_ref), channel_id=1, source_target_pairs={{0,8},{8,0},{16,24},{24,16},{1,9},{9,1},{17,25},{25,17},{2,10},{10... | collective-permute-start | bytes 3080 | tf_op jit(solution)/shard_map/ppermute | solution.py:370
  29.1 0.8 %collective-permute-start.7 = (f32[1,256]{1,0:T(1,128)S(1)}, f32[1,256]{1,0:T(1,128)S(1)}, u32[]{:S(2)}, u32[]{:S(2)}) collective-permute-start(f32[1,256]{1,0:T(1,128)S(1)} %get-tuple-element.29.own_ref), channel_id=1, source_target_pairs={{0,16},{8,24},{16,0},{24,8},{1,17},{9,25},{17,1},{25,9},{2,18},{10... | collective-permute-start | bytes 3080 | tf_op jit(solution)/shard_map/ppermute | solution.py:370
  29.9 0.7 %collective-permute-start.8 = (f32[1,256]{1,0:T(1,128)S(1)}, f32[1,256]{1,0:T(1,128)S(1)}, u32[]{:S(2)}, u32[]{:S(2)}) collective-permute-start(f32[1,256]{1,0:T(1,128)S(1)} %get-tuple-element.29.own_ref), channel_id=1, source_target_pairs={{0,24},{8,16},{16,8},{24,0},{1,25},{9,17},{17,9},{25,1},{2,26},{10... | collective-permute-start | bytes 3080 | tf_op jit(solution)/shard_map/ppermute | solution.py:370
  30.6 4.8 %gradient.1 = (bf16[19008,256]{1,0:T(8,128)(2,1)}, f32[1,256]{1,0:T(1,128)}) custom-call(s32[27]{0:T(128)S(1)} %get-tuple-element.19.flag_ref, f32[1,256]{1,0:T(1,128)S(1)} %get-tuple-element.30.lse_ref, f32[1,256]{1,0:T(1,128)S(1)} %get-tuple-element.29.own_ref, s32[64,256]{1,0:T(8,128)S(1)} %get-tuple-element.21.local_ref, ...), custom_call_target="tpu_custom_call" | custom-call | tf_op jit(solution)/shard_map/gradient/pallas_call | solution.py:456
  35.4 0.0 collective-permute-done.6
  35.4 0.0 collective-permute-done.7
  35.4 0.0 collective-permute-done.8
  35.4 0.6 %add_reduce_fusion = f32[]{:T(128)} fusion(f32[1,256]{1,0:T(1,128)S(1)} %collective-permute-done.7, f32[1,256]{1,0:T(1,128)S(1)} %collective-permute-done.8, f32[1,256]{1,0:T(1,128)S(1)} %get-tuple-element.29.own_ref, f32[1,256]{1,0:T(1,128)S(1)} %collective-permute-done.6), kind=kLoop, calls=%fused_computation.12 | loop fusion | flops 1023 | bytes 4100 | tf_op jit(solution)/shard_map/reduce_sum | solution.py:475
  (4 shorter events, 0.0 us)
Async XLA Ops:
  0.6 10.9 %copy-start = (s32[256,64]{0,1:T(8,128)S(1)}, s32[256,64]{0,1:T(8,128)}, u32[]{:S(2)}) copy-start(s32[256,64]{0,1:T(8,128)} %param.7) | copy-start | bytes 196612
  1.6 9.9 %collective-permute-start = (f32[72,256]{1,0:T(8,128)S(1)}, f32[72,256]{1,0:T(8,128)S(1)}, u32[]{:S(2)}, u32[]{:S(2)}) collective-permute-start(f32[72,256]{1,0:T(8,128)S(1)} %prepare.1.refs_0_), channel_id=1, source_target_pairs={{0,8},{8,0},{16,24},{24,16},{1,9},{9,1},{17,25},{25,17},{2,10},{10... | collective-permute-start | bytes 221192 | tf_op jit(solution)/shard_map/ppermute | solution.py:370
  4.6 6.9 %collective-permute-start.1 = (f32[72,256]{1,0:T(8,128)S(1)}, f32[72,256]{1,0:T(8,128)S(1)}, u32[]{:S(2)}, u32[]{:S(2)}) collective-permute-start(f32[72,256]{1,0:T(8,128)S(1)} %prepare.1.refs_0_), channel_id=1, source_target_pairs={{0,16},{8,24},{16,0},{24,8},{1,17},{9,25},{17,1},{25,9},{2,18},{10... | collective-permute-start | bytes 221192 | tf_op jit(solution)/shard_map/ppermute | solution.py:370
  6.1 5.3 %collective-permute-start.2 = (f32[72,256]{1,0:T(8,128)S(1)}, f32[72,256]{1,0:T(8,128)S(1)}, u32[]{:S(2)}, u32[]{:S(2)}) collective-permute-start(f32[72,256]{1,0:T(8,128)S(1)} %prepare.1.refs_0_), channel_id=1, source_target_pairs={{0,24},{8,16},{16,8},{24,0},{1,25},{9,17},{17,9},{25,1},{2,26},{10... | collective-permute-start | bytes 221192 | tf_op jit(solution)/shard_map/ppermute | solution.py:370
  16.7 1.2 %collective-permute-start.3 = (f32[8,256]{1,0:T(8,128)S(1)}, f32[8,256]{1,0:T(8,128)S(1)}, u32[]{:S(2)}, u32[]{:S(2)}) collective-permute-start(f32[8,256]{1,0:T(8,128)S(1)} %get-tuple-element.20), channel_id=1, source_target_pairs={{0,1},{1,0},{2,3},{3,2},{4,5},{5,4},{6,7},{7,6},{8,9},{9,8},{10,11... | collective-permute-start | bytes 24584 | tf_op jit(solution)/shard_map/ppermute | solution.py:450
  18.0 3.7 %collective-permute-start.4 = (f32[8,256]{1,0:T(8,128)S(1)}, f32[8,256]{1,0:T(8,128)S(1)}, u32[]{:S(2)}, u32[]{:S(2)}) collective-permute-start(f32[8,256]{1,0:T(8,128)S(1)} %maximum_maximum_fusion), channel_id=1, source_target_pairs={{0,2},{1,3},{2,0},{3,1},{4,6},{5,7},{6,4},{7,5},{8,10},{9,11},{10,... | collective-permute-start | bytes 24584 | tf_op jit(solution)/shard_map/ppermute | solution.py:450
  21.8 5.0 %collective-permute-start.5 = (f32[8,256]{1,0:T(8,128)S(1)}, f32[8,256]{1,0:T(8,128)S(1)}, u32[]{:S(2)}, u32[]{:S(2)}) collective-permute-start(f32[8,256]{1,0:T(8,128)S(1)} %maximum_maximum_fusion.1), channel_id=1, source_target_pairs={{0,4},{1,5},{2,6},{3,7},{4,0},{5,1},{6,2},{7,3},{8,12},{9,13},{10,... | collective-permute-start | bytes 24584 | tf_op jit(solution)/shard_map/ppermute | solution.py:450
  26.8 8.6 %collective-permute-start.6 = (f32[1,256]{1,0:T(1,128)S(1)}, f32[1,256]{1,0:T(1,128)S(1)}, u32[]{:S(2)}, u32[]{:S(2)}) collective-permute-start(f32[1,256]{1,0:T(1,128)S(1)} %get-tuple-element.29.own_ref), channel_id=1, source_target_pairs={{0,8},{8,0},{16,24},{24,16},{1,9},{9,1},{17,25},{25,17},{2,10},{10... | collective-permute-start | bytes 3080 | tf_op jit(solution)/shard_map/ppermute | solution.py:370
  29.1 6.3 %collective-permute-start.7 = (f32[1,256]{1,0:T(1,128)S(1)}, f32[1,256]{1,0:T(1,128)S(1)}, u32[]{:S(2)}, u32[]{:S(2)}) collective-permute-start(f32[1,256]{1,0:T(1,128)S(1)} %get-tuple-element.29.own_ref), channel_id=1, source_target_pairs={{0,16},{8,24},{16,0},{24,8},{1,17},{9,25},{17,1},{25,9},{2,18},{10... | collective-permute-start | bytes 3080 | tf_op jit(solution)/shard_map/ppermute | solution.py:370
  29.9 5.5 %collective-permute-start.8 = (f32[1,256]{1,0:T(1,128)S(1)}, f32[1,256]{1,0:T(1,128)S(1)}, u32[]{:S(2)}, u32[]{:S(2)}) collective-permute-start(f32[1,256]{1,0:T(1,128)S(1)} %get-tuple-element.29.own_ref), channel_id=1, source_target_pairs={{0,24},{8,16},{16,8},{24,0},{1,25},{9,17},{17,9},{25,1},{2,26},{10... | collective-permute-start | bytes 3080 | tf_op jit(solution)/shard_map/ppermute | solution.py:370

commit v5 on v4

--- a/solution.py
+++ b/solution.py
@@ -10,7 +10,7 @@
 
 LOG2E = 1.4426950408889634
 LANE_ROWS = 16
-DEPTH = 3
+DEPTH = 4
 UNROLL = 4
 CHAINS = 4
 USUAL = 2
@@ -178,20 +178,15 @@
         )
     targets_ref[...] = parts[:children] + parts[children : 2 * children] + parts[2 * children :]
 
-    third = jnp.where(depth >= USUAL, at_bucket.astype(f32), -1.0)
-    last = jnp.max(third).astype(jnp.int32)
-    third = jnp.where(depth >= USUAL, at_bucket.astype(f32), 1.0 * buckets)
-    first = jnp.min(third).astype(jnp.int32)
     for b in range(buckets):
-        flag_ref[b] = jnp.where((first <= b) & (last >= b), 1, 0).astype(jnp.int32)
-
-    @pl.when(deepest >= DEPTH)
+        flag_ref[b] = 0
+
+    @pl.when(deepest >= USUAL)
     def _():
-        for g in range(groups):
-            over = (depth >= DEPTH) & (slot >= g * slots) & (slot < (g + 1) * slots)
-            flag = jnp.max(jnp.where(over, 1.0, 0.0)).astype(jnp.int32)
-            for b in range(g * group, (g + 1) * group):
-                flag_ref[b] = jnp.where(flag > 0, 2, flag_ref[b])
+        for b in range(buckets):
+            most = jnp.max(jnp.where(at_bucket == b, depth, -1).astype(f32)).astype(jnp.int32)
+            deeper = jnp.where(most >= USUAL, 1, 0).astype(jnp.int32)
+            flag_ref[b] = jnp.where(most >= DEPTH, 2, deeper).astype(jnp.int32)
 
     steps = [(count + UNROLL - 1) // UNROLL for count in counts]
     for k in range(DEPTH):
@@ -246,7 +241,16 @@
 
     @pl.when(deepest >= USUAL)
     def _():
-        lax.fori_loop(0, groups, functools.partial(fill, levels=tuple(range(USUAL, DEPTH))), 0)
+        def deepen(g, unused):
+            flags = [flag_ref[g * group + b] for b in range(group)]
+
+            @pl.when(sum(flags) > 0)
+            def _():
+                fill(g, 0, tuple(range(USUAL, DEPTH)))
+
+            return unused
+
+        lax.fori_loop(0, groups, deepen, 0)
 
     out_ref[...] = stats_ref[...]
 
@@ -400,7 +404,7 @@
     )
     routed = [leaf] + shifted(leaf, "dp", groups)
 
-    bucket = largest_block(columns, 704)
+    bucket = largest_block(columns, 1584)
     buckets = columns // bucket
     group = 3 if buckets % 3 == 0 else 1
     stats, x, power, tops = pl.pallas_call(
@@ -451,7 +455,8 @@
         hop *= 2
     lse = sums[0:1] + jnp.log(sums[1:2])
     own = lse - sums[2:3]
-    others = shifted(own, "dp", groups)
+    portion = own / (groups * lanes)
+    others = shifted(portion, "dp", groups)
 
     gradient, row_loss = pl.pallas_call(
         functools.partial(gradient_kernel, bucket),
@@ -469,10 +474,10 @@
         compiler_params=params,
         name="gradient",
     )(flags, lse, own, local, targets, index, share, value, power, tops)
-    losses = [own] + others
+    losses = [portion] + others
     while len(losses) > 1:
         losses = [losses[i] + losses[i + 1] for i in range(0, len(losses), 2)]
-    mean_loss = jnp.sum(losses[0]) / (groups * lanes)
+    mean_loss = jnp.sum(losses[0])
     return gradient.T, row_loss.reshape(lanes), mean_loss
 
 

time: 37.9 us -> 35.1 us (0.926)
  between operations: 2.53 us -> 0.74 us
  Pallas kernels: 16.2 us -> 14.9 us
  waiting for transfers between devices: 4.35 us -> 5.02 us
    pallas_call x1, Pallas kernels: 5.21 us -> 4.18 us  [body(): pl.pallas_call(functools.partial(lists_kernel, groups, bucket, group), ou...]
    ppermute x3, waiting for transfers between devices: 4.33 us -> 4.99 us  [body(): sums = merge(sums, lax.ppermute(sums, 'tensor', pairs))]
  transfers between devices with their start and end apart: 9 -> 9, of which waited for: 3 -> 3; matrix products, arithmetic and copies ran while one was open for 0% -> 0% of each run, Pallas kernels for 27% -> 28%
where the time goes in v5:
time: 35.1 us; the launch traced here: 35.2 us
  Pallas kernels  14.9 us (42%)
  starting transfers between devices  13.7 us (39%)
  waiting for transfers between devices  5.02 us (14%)
  other arithmetic  0.79 us (2%)
  between operations  0.74 us (2%)
    ppermute x6, starting transfers between devices, shifted(): result.append(lax.ppermute(value, axis, pairs))  8.49 us
    pallas_call x1, Pallas kernels, body(): pl.pallas_call(functools.partial(stats_kernel, bucket), out_shape=(jax.Sh...  5.19 us
    ppermute x3, starting transfers between devices, body(): sums = merge(sums, lax.ppermute(sums, 'tensor', pairs))  5.16 us
    ppermute x3, waiting for transfers between devices, body(): sums = merge(sums, lax.ppermute(sums, 'tensor', pairs))  4.99 us
    pallas_call x1, Pallas kernels, body(): pl.pallas_call(functools.partial(gradient_kernel, bucket), out_shape=(jax...  4.58 us
    pallas_call x1, Pallas kernels, body(): pl.pallas_call(functools.partial(lists_kernel, groups, bucket, group), ou...  4.18 us
    pallas_call x1, Pallas kernels, body(): pl.pallas_call(prepare_kernel, out_shape=jax.ShapeDtypeStruct((children +...  0.93 us
  transfers between devices with their start and end apart: 9, of which 3 were waited for; matrix products, arithmetic and copies ran while one was open for 0% of the time, Pallas kernels for 28%

profile of v5, /device:TPU:0, one launch (start us, length us, event | category | flops | bytes accessed | tf_op | source)
XLA Modules:
  0.0 35.2 jit_solution(9430648766408948762)
XLA Ops:
  0.6 0.0 copy-start
  0.6 0.9 %prepare.1.refs_0_ = f32[72,256]{1,0:T(8,128)S(1)} custom-call(s32[64,256]{1,0:T(8,128)} %bitcast.10, s32[1,256]{1,0:T(1,128)} %bitcast.11, f32[1,256]{1,0:T(1,128)} %bitcast.12, s32[1,256]{1,0:T(1,128)} %bitcast.13), custom_call_target="tpu_custom_call" | custom-call | tf_op jit(solution)/shard_map/prepare/pallas_call | solution.py:394
  1.6 3.0 %collective-permute-start = (f32[72,256]{1,0:T(8,128)S(1)}, f32[72,256]{1,0:T(8,128)S(1)}, u32[]{:S(2)}, u32[]{:S(2)}) collective-permute-start(f32[72,256]{1,0:T(8,128)S(1)} %prepare.1.refs_0_), channel_id=1, source_target_pairs={{0,8},{8,0},{16,24},{24,16},{1,9},{9,1},{17,25},{25,17},{2,10},{10... | collective-permute-start | bytes 221192 | tf_op jit(solution)/shard_map/ppermute | solution.py:374
  4.6 1.5 %collective-permute-start.1 = (f32[72,256]{1,0:T(8,128)S(1)}, f32[72,256]{1,0:T(8,128)S(1)}, u32[]{:S(2)}, u32[]{:S(2)}) collective-permute-start(f32[72,256]{1,0:T(8,128)S(1)} %prepare.1.refs_0_), channel_id=1, source_target_pairs={{0,16},{8,24},{16,0},{24,8},{1,17},{9,25},{17,1},{25,9},{2,18},{10... | collective-permute-start | bytes 221192 | tf_op jit(solution)/shard_map/ppermute | solution.py:374
  6.1 0.0 collective-permute-start.2
  6.2 5.2 %stats.1 = (f32[8,256]{1,0:T(8,128)S(1)}, bf16[19008,256]{1,0:T(8,128)(2,1)S(1)}, f32[19008,256]{1,0:T(8,128)S(1)}, f32[192,256]{1,0:T(8,128)S(1)}) custom-call(bf16[19008,256]{1,0:T(8,128)(2,1)} %bitcast.9), custom_call_target="tpu_custom_call" | custom-call | tf_op jit(solution)/shard_map/stats/pallas_call | solution.py:410
  11.3 0.0 collective-permute-done.refs_1_
  11.4 0.0 collective-permute-done.1.refs_2_
  11.4 0.0 collective-permute-done.2.refs_3_
  11.4 0.0 copy-done
  11.4 4.2 %lists.1 = (s32[64,256]{1,0:T(8,128)S(1)}, f32[64,256]{1,0:T(8,128)S(1)}, bf16[4,192,256]{2,1,0:T(8,128)(2,1)S(1)}, f32[4,192,256]{2,1,0:T(8,128)S(1)}, bf16[4,1...) custom-call(f32[72,256]{1,0:T(8,128)S(1)} %prepare.1.refs_0_, ...), custom_call_target="tpu_custom_call" | custom-call | tf_op jit(solution)/shard_map/lists/pallas_call | solution.py:427
  15.6 0.1 collective-permute-start.3
  15.7 0.1 pad.7.clone
  15.7 1.1 %collective-permute-done.3 = f32[8,256]{1,0:T(8,128)S(1)} collective-permute-done((f32[8,256]{1,0:T(8,128)S(1)}, f32[8,256]{1,0:T(8,128)S(1)}, u32[]{:S(2)}, u32[]{:S(2)}) %collective-permute-start.3) | collective-permute-done | bytes 8224 | tf_op jit(solution)/shard_map/ppermute | solution.py:454
  16.8 0.1 maximum_maximum_fusion
  16.9 2.8 %collective-permute-start.4 = (f32[8,256]{1,0:T(8,128)S(1)}, f32[8,256]{1,0:T(8,128)S(1)}, u32[]{:S(2)}, u32[]{:S(2)}) collective-permute-start(f32[8,256]{1,0:T(8,128)S(1)} %maximum_maximum_fusion), channel_id=1, source_target_pairs={{0,2},{1,3},{2,0},{3,1},{4,6},{5,7},{6,4},{7,5},{8,10},{9,11},{10,... | collective-permute-start | bytes 24584 | tf_op jit(solution)/shard_map/ppermute | solution.py:454
  19.7 1.6 %collective-permute-done.4 = f32[8,256]{1,0:T(8,128)S(1)} collective-permute-done((f32[8,256]{1,0:T(8,128)S(1)}, f32[8,256]{1,0:T(8,128)S(1)}, u32[]{:S(2)}, u32[]{:S(2)}) %collective-permute-start.4) | collective-permute-done | bytes 8224 | tf_op jit(solution)/shard_map/ppermute | solution.py:454
  21.4 0.1 maximum_maximum_fusion.1
  21.4 2.3 %collective-permute-start.5 = (f32[8,256]{1,0:T(8,128)S(1)}, f32[8,256]{1,0:T(8,128)S(1)}, u32[]{:S(2)}, u32[]{:S(2)}) collective-permute-start(f32[8,256]{1,0:T(8,128)S(1)} %maximum_maximum_fusion.1), channel_id=1, source_target_pairs={{0,4},{1,5},{2,6},{3,7},{4,0},{5,1},{6,2},{7,3},{8,12},{9,13},{10,... | collective-permute-start | bytes 24584 | tf_op jit(solution)/shard_map/ppermute | solution.py:454
  23.7 2.3 %collective-permute-done.5 = f32[8,256]{1,0:T(8,128)S(1)} collective-permute-done((f32[8,256]{1,0:T(8,128)S(1)}, f32[8,256]{1,0:T(8,128)S(1)}, u32[]{:S(2)}, u32[]{:S(2)}) %collective-permute-start.5) | collective-permute-done | bytes 8224 | tf_op jit(solution)/shard_map/ppermute | solution.py:454
  26.0 1.5 %collective-permute-start.6 = (f32[1,256]{1,0:T(1,128)S(1)}, f32[1,256]{1,0:T(1,128)S(1)}, u32[]{:S(2)}, u32[]{:S(2)}) collective-permute-start(f32[1,256]{1,0:T(1,128)S(1)} %get-tuple-element.29), channel_id=1, source_target_pairs={{0,8},{8,0},{16,24},{24,16},{1,9},{9,1},{17,25},{25,17},{2,10},{10... | collective-permute-start | bytes 3080 | tf_op jit(solution)/shard_map/ppermute | solution.py:374
  27.5 2.4 %collective-permute-start.7 = (f32[1,256]{1,0:T(1,128)S(1)}, f32[1,256]{1,0:T(1,128)S(1)}, u32[]{:S(2)}, u32[]{:S(2)}) collective-permute-start(f32[1,256]{1,0:T(1,128)S(1)} %get-tuple-element.29), channel_id=1, source_target_pairs={{0,16},{8,24},{16,0},{24,8},{1,17},{9,25},{17,1},{25,9},{2,18},{10... | collective-permute-start | bytes 3080 | tf_op jit(solution)/shard_map/ppermute | solution.py:374
  29.9 0.0 collective-permute-start.8
  29.9 4.6 %gradient.1 = (bf16[19008,256]{1,0:T(8,128)(2,1)}, f32[1,256]{1,0:T(1,128)}) custom-call(s32[12]{0:T(128)S(1)} %get-tuple-element.19.flag_ref, f32[1,256]{1,0:T(1,128)S(1)} %get-tuple-element.31.lse_ref, f32[1,256]{1,0:T(1,128)S(1)} %get-tuple-element.30.own_ref, s32[64,256]{1,0:T(8,128)S(1)} %get-tuple-element.21.local_ref, ...), custom_call_target="tpu_custom_call" | custom-call | tf_op jit(solution)/shard_map/gradient/pallas_call | solution.py:461
  34.5 0.0 collective-permute-done.6
  34.5 0.0 collective-permute-done.7
  34.5 0.0 collective-permute-done.8
  34.6 0.6 %add_reduce_fusion = f32[]{:T(128)} fusion(f32[1,256]{1,0:T(1,128)S(1)} %collective-permute-done.7, f32[1,256]{1,0:T(1,128)S(1)} %collective-permute-done.8, f32[1,256]{1,0:T(1,128)S(1)} %collective-permute-done.6, f32[1,256]{1,0:T(1,128)S(1)} %get-tuple-element.30.own_ref), kind=kLoop, calls=%fused_computation.12 | loop fusion | flops 1279 | bytes 4100 | tf_op jit(solution)/shard_map/reduce_sum | solution.py:480
  (4 shorter events, 0.0 us)
Async XLA Ops:
  0.6 10.8 %copy-start = (s32[256,64]{0,1:T(8,128)S(1)}, s32[256,64]{0,1:T(8,128)}, u32[]{:S(2)}) copy-start(s32[256,64]{0,1:T(8,128)} %param.7) | copy-start | bytes 196612
  1.6 9.8 %collective-permute-start = (f32[72,256]{1,0:T(8,128)S(1)}, f32[72,256]{1,0:T(8,128)S(1)}, u32[]{:S(2)}, u32[]{:S(2)}) collective-permute-start(f32[72,256]{1,0:T(8,128)S(1)} %prepare.1.refs_0_), channel_id=1, source_target_pairs={{0,8},{8,0},{16,24},{24,16},{1,9},{9,1},{17,25},{25,17},{2,10},{10... | collective-permute-start | bytes 221192 | tf_op jit(solution)/shard_map/ppermute | solution.py:374
  4.6 6.7 %collective-permute-start.1 = (f32[72,256]{1,0:T(8,128)S(1)}, f32[72,256]{1,0:T(8,128)S(1)}, u32[]{:S(2)}, u32[]{:S(2)}) collective-permute-start(f32[72,256]{1,0:T(8,128)S(1)} %prepare.1.refs_0_), channel_id=1, source_target_pairs={{0,16},{8,24},{16,0},{24,8},{1,17},{9,25},{17,1},{25,9},{2,18},{10... | collective-permute-start | bytes 221192 | tf_op jit(solution)/shard_map/ppermute | solution.py:374
  6.1 5.3 %collective-permute-start.2 = (f32[72,256]{1,0:T(8,128)S(1)}, f32[72,256]{1,0:T(8,128)S(1)}, u32[]{:S(2)}, u32[]{:S(2)}) collective-permute-start(f32[72,256]{1,0:T(8,128)S(1)} %prepare.1.refs_0_), channel_id=1, source_target_pairs={{0,24},{8,16},{16,8},{24,0},{1,25},{9,17},{17,9},{25,1},{2,26},{10... | collective-permute-start | bytes 221192 | tf_op jit(solution)/shard_map/ppermute | solution.py:374
  15.6 1.2 %collective-permute-start.3 = (f32[8,256]{1,0:T(8,128)S(1)}, f32[8,256]{1,0:T(8,128)S(1)}, u32[]{:S(2)}, u32[]{:S(2)}) collective-permute-start(f32[8,256]{1,0:T(8,128)S(1)} %get-tuple-element.20), channel_id=1, source_target_pairs={{0,1},{1,0},{2,3},{3,2},{4,5},{5,4},{6,7},{7,6},{8,9},{9,8},{10,11... | collective-permute-start | bytes 24584 | tf_op jit(solution)/shard_map/ppermute | solution.py:454
  16.9 4.4 %collective-permute-start.4 = (f32[8,256]{1,0:T(8,128)S(1)}, f32[8,256]{1,0:T(8,128)S(1)}, u32[]{:S(2)}, u32[]{:S(2)}) collective-permute-start(f32[8,256]{1,0:T(8,128)S(1)} %maximum_maximum_fusion), channel_id=1, source_target_pairs={{0,2},{1,3},{2,0},{3,1},{4,6},{5,7},{6,4},{7,5},{8,10},{9,11},{10,... | collective-permute-start | bytes 24584 | tf_op jit(solution)/shard_map/ppermute | solution.py:454
  21.4 4.6 %collective-permute-start.5 = (f32[8,256]{1,0:T(8,128)S(1)}, f32[8,256]{1,0:T(8,128)S(1)}, u32[]{:S(2)}, u32[]{:S(2)}) collective-permute-start(f32[8,256]{1,0:T(8,128)S(1)} %maximum_maximum_fusion.1), channel_id=1, source_target_pairs={{0,4},{1,5},{2,6},{3,7},{4,0},{5,1},{6,2},{7,3},{8,12},{9,13},{10,... | collective-permute-start | bytes 24584 | tf_op jit(solution)/shard_map/ppermute | solution.py:454
  26.0 8.5 %collective-permute-start.6 = (f32[1,256]{1,0:T(1,128)S(1)}, f32[1,256]{1,0:T(1,128)S(1)}, u32[]{:S(2)}, u32[]{:S(2)}) collective-permute-start(f32[1,256]{1,0:T(1,128)S(1)} %get-tuple-element.29), channel_id=1, source_target_pairs={{0,8},{8,0},{16,24},{24,16},{1,9},{9,1},{17,25},{25,17},{2,10},{10... | collective-permute-start | bytes 3080 | tf_op jit(solution)/shard_map/ppermute | solution.py:374
  27.5 7.0 %collective-permute-start.7 = (f32[1,256]{1,0:T(1,128)S(1)}, f32[1,256]{1,0:T(1,128)S(1)}, u32[]{:S(2)}, u32[]{:S(2)}) collective-permute-start(f32[1,256]{1,0:T(1,128)S(1)} %get-tuple-element.29), channel_id=1, source_target_pairs={{0,16},{8,24},{16,0},{24,8},{1,17},{9,25},{17,1},{25,9},{2,18},{10... | collective-permute-start | bytes 3080 | tf_op jit(solution)/shard_map/ppermute | solution.py:374
  29.9 4.6 %collective-permute-start.8 = (f32[1,256]{1,0:T(1,128)S(1)}, f32[1,256]{1,0:T(1,128)S(1)}, u32[]{:S(2)}, u32[]{:S(2)}) collective-permute-start(f32[1,256]{1,0:T(1,128)S(1)} %get-tuple-element.29), channel_id=1, source_target_pairs={{0,24},{8,16},{16,8},{24,0},{1,25},{9,17},{17,9},{25,1},{2,26},{10... | collective-permute-start | bytes 3080 | tf_op jit(solution)/shard_map/ppermute | solution.py:374

commit v6 on v5

--- a/solution.py
+++ b/solution.py
@@ -13,6 +13,7 @@
 DEPTH = 4
 UNROLL = 4
 CHAINS = 4
+PIECES = 3
 USUAL = 2
 VMEM_BYTES = 13 * 1024 * 1024
 
@@ -92,7 +93,10 @@
     copy(0).wait()
     first = view(x_ref, 0)
     tops = [first[i * LANE_ROWS : (i + 1) * LANE_ROWS, :] for i in range(units)]
-    top = functools.reduce(jnp.maximum, tops)
+    chains = tops[:CHAINS]
+    for i in range(CHAINS, units):
+        chains[i % CHAINS] = jnp.maximum(chains[i % CHAINS], tops[i])
+    top = functools.reduce(jnp.maximum, chains)
     top, acc = lax.fori_loop(0, blocks - 1, one, (top, jnp.zeros((LANE_ROWS, lanes), jnp.float32)))
     wide = top.astype(jnp.float32)
     acc, _ = block_pass(blocks - 1, wide, acc, None, top)
@@ -314,8 +318,12 @@
     total, lanes = power_ref.shape
     buckets = total // bucket
 
+    units = bucket // LANE_ROWS
+    pieces = PIECES if units % PIECES == 0 else 1
+    piece = bucket // pieces
+
     def back(index):
-        window = pl.ds(index * bucket, bucket)
+        window = pl.ds(index * piece, piece)
         return pltpu.make_async_copy(out_ref.at[window, :], out_hbm.at[window, :], sems.at[index])
 
     losses = pltpu.make_async_copy(own_ref, loss_hbm, loss_sem)
@@ -336,13 +344,15 @@
                 given.append((soft - share_ref[k, at, :]).astype(jnp.bfloat16))
             powers = power_ref.at[pl.ds(base, bucket), :]
             results = out_ref.at[pl.ds(base, bucket), :]
-            for i in range(bucket // LANE_ROWS):
+            for i in range(units):
                 row = slice(i * LANE_ROWS, (i + 1) * LANE_ROWS)
                 result = (powers[row, :] * scale).astype(jnp.bfloat16)
                 mark = jnp.bfloat16(i)
                 for k in range(entries):
                     result = jnp.where(index[k] == mark, given[k], result)
                 results[row, :] = result
+                if (i + 1) % (units // pieces) == 0:
+                    back(b * pieces + i // (units // pieces)).start()
 
         pl.when(flag_ref[b] == 0)(functools.partial(listed, USUAL))
         pl.when(flag_ref[b] == 1)(functools.partial(listed, DEPTH))
@@ -356,13 +366,14 @@
                 out_ref[row, :] = (power_ref[row, :] * scale - dense).astype(jnp.bfloat16)
                 return unused
 
-            lax.fori_loop(0, bucket // LANE_ROWS, fill, 0)
-
-        back(b).start()
+            lax.fori_loop(0, units, fill, 0)
+            for part in range(pieces):
+                back(b * pieces + part).start()
+
         return carry
 
     lax.fori_loop(0, buckets, one, 0)
-    for index in range(buckets):
+    for index in range(buckets * pieces):
         back(index).wait()
     losses.wait()
 
@@ -468,7 +479,7 @@
         out_specs=(any_spec(), any_spec()),
         scratch_shapes=[
             pltpu.VMEM((columns, lanes), jnp.bfloat16),
-            pltpu.SemaphoreType.DMA((buckets,)),
+            pltpu.SemaphoreType.DMA((buckets * PIECES,)),
             pltpu.SemaphoreType.DMA(()),
         ],
         compiler_params=params,

time: 35.1 us -> 34.8 us (level)
  waiting for transfers between devices: 5.02 us -> 4.36 us
    ppermute x3, waiting for transfers between devices: 4.99 us -> 4.33 us  [body(): sums = merge(sums, lax.ppermute(sums, 'tensor', pairs))]
where the time goes in v6:
time: 34.8 us; the launch traced here: 34.6 us
  Pallas kernels  14.9 us (43%)
  starting transfers between devices  13.7 us (39%)
  waiting for transfers between devices  4.36 us (13%)
  other arithmetic  0.79 us (2%)
  between operations  0.74 us (2%)
    ppermute x6, starting transfers between devices, shifted(): result.append(lax.ppermute(value, axis, pairs))  8.27 us
    ppermute x3, starting transfers between devices, body(): sums = merge(sums, lax.ppermute(sums, 'tensor', pairs))  5.48 us
    pallas_call x1, Pallas kernels, body(): pl.pallas_call(functools.partial(stats_kernel, bucket), out_shape=(jax.Sh...  5.19 us
    pallas_call x1, Pallas kernels, body(): pl.pallas_call(functools.partial(gradient_kernel, bucket), out_shape=(jax...  4.61 us
    ppermute x3, waiting for transfers between devices, body(): sums = merge(sums, lax.ppermute(sums, 'tensor', pairs))  4.33 us
    pallas_call x1, Pallas kernels, body(): pl.pallas_call(functools.partial(lists_kernel, groups, bucket, group), ou...  4.18 us
    pallas_call x1, Pallas kernels, body(): pl.pallas_call(prepare_kernel, out_shape=jax.ShapeDtypeStruct((children +...  0.93 us
  transfers between devices with their start and end apart: 9, of which 3 were waited for; matrix products, arithmetic and copies ran while one was open for 0% of the time, Pallas kernels for 28%

profile of v6, /device:TPU:0, one launch (start us, length us, event | category | flops | bytes accessed | tf_op | source)
XLA Modules:
  0.0 34.6 jit_solution(4367938868250841834)
XLA Ops:
  0.6 0.0 copy-start
  0.6 0.9 %prepare.1.refs_0_ = f32[72,256]{1,0:T(8,128)S(1)} custom-call(s32[64,256]{1,0:T(8,128)} %bitcast.10, s32[1,256]{1,0:T(1,128)} %bitcast.11, f32[1,256]{1,0:T(1,128)} %bitcast.12, s32[1,256]{1,0:T(1,128)} %bitcast.13), custom_call_target="tpu_custom_call" | custom-call | tf_op jit(solution)/shard_map/prepare/pallas_call | solution.py:405
  1.6 3.0 %collective-permute-start = (f32[72,256]{1,0:T(8,128)S(1)}, f32[72,256]{1,0:T(8,128)S(1)}, u32[]{:S(2)}, u32[]{:S(2)}) collective-permute-start(f32[72,256]{1,0:T(8,128)S(1)} %prepare.1.refs_0_), channel_id=1, source_target_pairs={{0,8},{8,0},{16,24},{24,16},{1,9},{9,1},{17,25},{25,17},{2,10},{10... | collective-permute-start | bytes 221192 | tf_op jit(solution)/shard_map/ppermute | solution.py:385
  4.6 1.5 %collective-permute-start.1 = (f32[72,256]{1,0:T(8,128)S(1)}, f32[72,256]{1,0:T(8,128)S(1)}, u32[]{:S(2)}, u32[]{:S(2)}) collective-permute-start(f32[72,256]{1,0:T(8,128)S(1)} %prepare.1.refs_0_), channel_id=1, source_target_pairs={{0,16},{8,24},{16,0},{24,8},{1,17},{9,25},{17,1},{25,9},{2,18},{10... | collective-permute-start | bytes 221192 | tf_op jit(solution)/shard_map/ppermute | solution.py:385
  6.1 0.0 collective-permute-start.2
  6.2 5.2 %stats.1 = (f32[8,256]{1,0:T(8,128)S(1)}, bf16[19008,256]{1,0:T(8,128)(2,1)S(1)}, f32[19008,256]{1,0:T(8,128)S(1)}, f32[192,256]{1,0:T(8,128)S(1)}) custom-call(bf16[19008,256]{1,0:T(8,128)(2,1)} %bitcast.9), custom_call_target="tpu_custom_call" | custom-call | tf_op jit(solution)/shard_map/stats/pallas_call | solution.py:421
  11.3 0.0 collective-permute-done.refs_1_
  11.4 0.0 collective-permute-done.1.refs_2_
  11.4 0.0 collective-permute-done.2.refs_3_
  11.4 0.0 copy-done
  11.4 4.2 %lists.1 = (s32[64,256]{1,0:T(8,128)S(1)}, f32[64,256]{1,0:T(8,128)S(1)}, bf16[4,192,256]{2,1,0:T(8,128)(2,1)S(1)}, f32[4,192,256]{2,1,0:T(8,128)S(1)}, bf16[4,1...) custom-call(f32[72,256]{1,0:T(8,128)S(1)} %prepare.1.refs_0_, ...), custom_call_target="tpu_custom_call" | custom-call | tf_op jit(solution)/shard_map/lists/pallas_call | solution.py:438
  15.6 0.1 collective-permute-start.3
  15.7 0.1 pad.7.clone
  15.7 1.1 %collective-permute-done.3 = f32[8,256]{1,0:T(8,128)S(1)} collective-permute-done((f32[8,256]{1,0:T(8,128)S(1)}, f32[8,256]{1,0:T(8,128)S(1)}, u32[]{:S(2)}, u32[]{:S(2)}) %collective-permute-start.3) | collective-permute-done | bytes 8224 | tf_op jit(solution)/shard_map/ppermute | solution.py:465
  16.8 0.1 maximum_maximum_fusion
  16.9 2.2 %collective-permute-start.4 = (f32[8,256]{1,0:T(8,128)S(1)}, f32[8,256]{1,0:T(8,128)S(1)}, u32[]{:S(2)}, u32[]{:S(2)}) collective-permute-start(f32[8,256]{1,0:T(8,128)S(1)} %maximum_maximum_fusion), channel_id=1, source_target_pairs={{0,2},{1,3},{2,0},{3,1},{4,6},{5,7},{6,4},{7,5},{8,10},{9,11},{10,... | collective-permute-start | bytes 24584 | tf_op jit(solution)/shard_map/ppermute | solution.py:465
  19.1 1.6 %collective-permute-done.4 = f32[8,256]{1,0:T(8,128)S(1)} collective-permute-done((f32[8,256]{1,0:T(8,128)S(1)}, f32[8,256]{1,0:T(8,128)S(1)}, u32[]{:S(2)}, u32[]{:S(2)}) %collective-permute-start.4) | collective-permute-done | bytes 8224 | tf_op jit(solution)/shard_map/ppermute | solution.py:465
  20.8 0.1 maximum_maximum_fusion.1
  20.8 3.2 %collective-permute-start.5 = (f32[8,256]{1,0:T(8,128)S(1)}, f32[8,256]{1,0:T(8,128)S(1)}, u32[]{:S(2)}, u32[]{:S(2)}) collective-permute-start(f32[8,256]{1,0:T(8,128)S(1)} %maximum_maximum_fusion.1), channel_id=1, source_target_pairs={{0,4},{1,5},{2,6},{3,7},{4,0},{5,1},{6,2},{7,3},{8,12},{9,13},{10,... | collective-permute-start | bytes 24584 | tf_op jit(solution)/shard_map/ppermute | solution.py:465
  24.0 1.6 %collective-permute-done.5 = f32[8,256]{1,0:T(8,128)S(1)} collective-permute-done((f32[8,256]{1,0:T(8,128)S(1)}, f32[8,256]{1,0:T(8,128)S(1)}, u32[]{:S(2)}, u32[]{:S(2)}) %collective-permute-start.5) | collective-permute-done | bytes 8224 | tf_op jit(solution)/shard_map/ppermute | solution.py:465
  25.7 2.2 %collective-permute-start.6 = (f32[1,256]{1,0:T(1,128)S(1)}, f32[1,256]{1,0:T(1,128)S(1)}, u32[]{:S(2)}, u32[]{:S(2)}) collective-permute-start(f32[1,256]{1,0:T(1,128)S(1)} %get-tuple-element.29), channel_id=1, source_target_pairs={{0,8},{8,0},{16,24},{24,16},{1,9},{9,1},{17,25},{25,17},{2,10},{10... | collective-permute-start | bytes 3080 | tf_op jit(solution)/shard_map/ppermute | solution.py:385
  27.8 1.1 %collective-permute-start.7 = (f32[1,256]{1,0:T(1,128)S(1)}, f32[1,256]{1,0:T(1,128)S(1)}, u32[]{:S(2)}, u32[]{:S(2)}) collective-permute-start(f32[1,256]{1,0:T(1,128)S(1)} %get-tuple-element.29), channel_id=1, source_target_pairs={{0,16},{8,24},{16,0},{24,8},{1,17},{9,25},{17,1},{25,9},{2,18},{10... | collective-permute-start | bytes 3080 | tf_op jit(solution)/shard_map/ppermute | solution.py:385
  29.0 0.4 %collective-permute-start.8 = (f32[1,256]{1,0:T(1,128)S(1)}, f32[1,256]{1,0:T(1,128)S(1)}, u32[]{:S(2)}, u32[]{:S(2)}) collective-permute-start(f32[1,256]{1,0:T(1,128)S(1)} %get-tuple-element.29), channel_id=1, source_target_pairs={{0,24},{8,16},{16,8},{24,0},{1,25},{9,17},{17,9},{25,1},{2,26},{10... | collective-permute-start | bytes 3080 | tf_op jit(solution)/shard_map/ppermute | solution.py:385
  29.4 4.6 %gradient.1 = (bf16[19008,256]{1,0:T(8,128)(2,1)}, f32[1,256]{1,0:T(1,128)}) custom-call(s32[12]{0:T(128)S(1)} %get-tuple-element.19.flag_ref, f32[1,256]{1,0:T(1,128)S(1)} %get-tuple-element.31.lse_ref, f32[1,256]{1,0:T(1,128)S(1)} %get-tuple-element.30.own_ref, s32[64,256]{1,0:T(8,128)S(1)} %get-tuple-element.21.local_ref, ...), custom_call_target="tpu_custom_call" | custom-call | tf_op jit(solution)/shard_map/gradient/pallas_call | solution.py:472
  34.0 0.0 collective-permute-done.6
  34.0 0.0 collective-permute-done.7
  34.0 0.0 collective-permute-done.8
  34.0 0.6 %add_reduce_fusion = f32[]{:T(128)} fusion(f32[1,256]{1,0:T(1,128)S(1)} %collective-permute-done.7, f32[1,256]{1,0:T(1,128)S(1)} %collective-permute-done.8, f32[1,256]{1,0:T(1,128)S(1)} %collective-permute-done.6, f32[1,256]{1,0:T(1,128)S(1)} %get-tuple-element.30.own_ref), kind=kLoop, calls=%fused_computation.12 | loop fusion | flops 1279 | bytes 4100 | tf_op jit(solution)/shard_map/reduce_sum | solution.py:491
  (4 shorter events, 0.0 us)
Async XLA Ops:
  0.6 10.8 %copy-start = (s32[256,64]{0,1:T(8,128)S(1)}, s32[256,64]{0,1:T(8,128)}, u32[]{:S(2)}) copy-start(s32[256,64]{0,1:T(8,128)} %param.7) | copy-start | bytes 196612
  1.6 9.8 %collective-permute-start = (f32[72,256]{1,0:T(8,128)S(1)}, f32[72,256]{1,0:T(8,128)S(1)}, u32[]{:S(2)}, u32[]{:S(2)}) collective-permute-start(f32[72,256]{1,0:T(8,128)S(1)} %prepare.1.refs_0_), channel_id=1, source_target_pairs={{0,8},{8,0},{16,24},{24,16},{1,9},{9,1},{17,25},{25,17},{2,10},{10... | collective-permute-start | bytes 221192 | tf_op jit(solution)/shard_map/ppermute | solution.py:385
  4.6 6.7 %collective-permute-start.1 = (f32[72,256]{1,0:T(8,128)S(1)}, f32[72,256]{1,0:T(8,128)S(1)}, u32[]{:S(2)}, u32[]{:S(2)}) collective-permute-start(f32[72,256]{1,0:T(8,128)S(1)} %prepare.1.refs_0_), channel_id=1, source_target_pairs={{0,16},{8,24},{16,0},{24,8},{1,17},{9,25},{17,1},{25,9},{2,18},{10... | collective-permute-start | bytes 221192 | tf_op jit(solution)/shard_map/ppermute | solution.py:385
  6.1 5.3 %collective-permute-start.2 = (f32[72,256]{1,0:T(8,128)S(1)}, f32[72,256]{1,0:T(8,128)S(1)}, u32[]{:S(2)}, u32[]{:S(2)}) collective-permute-start(f32[72,256]{1,0:T(8,128)S(1)} %prepare.1.refs_0_), channel_id=1, source_target_pairs={{0,24},{8,16},{16,8},{24,0},{1,25},{9,17},{17,9},{25,1},{2,26},{10... | collective-permute-start | bytes 221192 | tf_op jit(solution)/shard_map/ppermute | solution.py:385
  15.6 1.2 %collective-permute-start.3 = (f32[8,256]{1,0:T(8,128)S(1)}, f32[8,256]{1,0:T(8,128)S(1)}, u32[]{:S(2)}, u32[]{:S(2)}) collective-permute-start(f32[8,256]{1,0:T(8,128)S(1)} %get-tuple-element.20), channel_id=1, source_target_pairs={{0,1},{1,0},{2,3},{3,2},{4,5},{5,4},{6,7},{7,6},{8,9},{9,8},{10,11... | collective-permute-start | bytes 24584 | tf_op jit(solution)/shard_map/ppermute | solution.py:465
  16.9 3.9 %collective-permute-start.4 = (f32[8,256]{1,0:T(8,128)S(1)}, f32[8,256]{1,0:T(8,128)S(1)}, u32[]{:S(2)}, u32[]{:S(2)}) collective-permute-start(f32[8,256]{1,0:T(8,128)S(1)} %maximum_maximum_fusion), channel_id=1, source_target_pairs={{0,2},{1,3},{2,0},{3,1},{4,6},{5,7},{6,4},{7,5},{8,10},{9,11},{10,... | collective-permute-start | bytes 24584 | tf_op jit(solution)/shard_map/ppermute | solution.py:465
  20.8 4.8 %collective-permute-start.5 = (f32[8,256]{1,0:T(8,128)S(1)}, f32[8,256]{1,0:T(8,128)S(1)}, u32[]{:S(2)}, u32[]{:S(2)}) collective-permute-start(f32[8,256]{1,0:T(8,128)S(1)} %maximum_maximum_fusion.1), channel_id=1, source_target_pairs={{0,4},{1,5},{2,6},{3,7},{4,0},{5,1},{6,2},{7,3},{8,12},{9,13},{10,... | collective-permute-start | bytes 24584 | tf_op jit(solution)/shard_map/ppermute | solution.py:465
  25.7 8.3 %collective-permute-start.6 = (f32[1,256]{1,0:T(1,128)S(1)}, f32[1,256]{1,0:T(1,128)S(1)}, u32[]{:S(2)}, u32[]{:S(2)}) collective-permute-start(f32[1,256]{1,0:T(1,128)S(1)} %get-tuple-element.29), channel_id=1, source_target_pairs={{0,8},{8,0},{16,24},{24,16},{1,9},{9,1},{17,25},{25,17},{2,10},{10... | collective-permute-start | bytes 3080 | tf_op jit(solution)/shard_map/ppermute | solution.py:385
  27.8 6.2 %collective-permute-start.7 = (f32[1,256]{1,0:T(1,128)S(1)}, f32[1,256]{1,0:T(1,128)S(1)}, u32[]{:S(2)}, u32[]{:S(2)}) collective-permute-start(f32[1,256]{1,0:T(1,128)S(1)} %get-tuple-element.29), channel_id=1, source_target_pairs={{0,16},{8,24},{16,0},{24,8},{1,17},{9,25},{17,1},{25,9},{2,18},{10... | collective-permute-start | bytes 3080 | tf_op jit(solution)/shard_map/ppermute | solution.py:385
  29.0 5.0 %collective-permute-start.8 = (f32[1,256]{1,0:T(1,128)S(1)}, f32[1,256]{1,0:T(1,128)S(1)}, u32[]{:S(2)}, u32[]{:S(2)}) collective-permute-start(f32[1,256]{1,0:T(1,128)S(1)} %get-tuple-element.29), channel_id=1, source_target_pairs={{0,24},{8,16},{16,8},{24,0},{1,25},{9,17},{17,9},{25,1},{2,26},{10... | collective-permute-start | bytes 3080 | tf_op jit(solution)/shard_map/ppermute | solution.py:385
